TPU v7x, 32 devices: a whole 2x2x4 slice. The times are simulated.
32 devices in a mesh: groups: 2 (over y), bank: 4 (over z), freq: 2 (over x), seg: 2 (over core).
Axes of the slice: x: 2, y: 2, z: 4, core: 2. Of those that a mesh axis runs over, the one named last changes fastest.
Arguments:
- coarse_spectra: bfloat16 [64, 2, 16384], P(('groups', 'seg', 'bank'), None, 'freq'), parts along dimension 0, may hold values from -6 to 6
- fine_spectra: bfloat16 [64, 2, 65536], P(('groups', 'seg', 'bank'), None, 'freq'), parts along dimension 0, may hold values from -6 to 6
- coarse_templates: bfloat16 [2, 2048, 16384], P(None, 'bank', 'freq'), may hold values from -6 to 6
- fine_templates: bfloat16 [2, 4, 64, 65536], P(None, 'bank', None, 'freq'), may hold values from -6 to 6
- coarse_weight: float32 [32768], P(('groups', 'freq')), parts along dimension 0, may hold values from 0.2 to 2
- fine_weight: float32 [131072], P(('groups', 'freq')), parts along dimension 0, may hold values from 0.2 to 2
- triggers: int32 [64, 2], P(('groups', 'seg')), parts along dimension 0, may hold values from 0 to 3, all different within a row; in each aligned block of 4 rows (0 to 3, 4 to 7, ...) at most 2 rows name the same one
- offsets: int32 [64, 2], P(('groups', 'seg')), parts along dimension 0, may hold values from 0 to 131056
Outputs:
- coarse_snr: float32 [2048, 64], P(('bank', 'freq'), ('groups', 'seg')), parts along dimension 1
- fine_snr: float32 [64, 2, 64], P(('groups', 'seg', 'bank'), None, 'freq'), parts along dimension 0
There are 2 independent parts, one for each index of `groups`. A program takes and returns all parts, laid end to end along the dimension named above; an argument that names none is the same for every part. Nothing has to cross between parts.
Inputs may be any that keep to these rules, and one draw needn't show every extreme that they name: `triggers`: each segment names 2 different sub-banks. In each aligned block of 4 segments (the segments of one device along seg and bank) no sub-bank is named more than 2 times.
All inputs are finite; a program needn't handle non-finite values.
Results may differ from a plain program's by a relative error of at most 0.0021.
Values may be sent and summed in bfloat16 or wider, within the bound.
No kernel may reach another device: no remote copies, remote signals or barrier semaphores. Data moves between devices by JAX's collectives and lax.ppermute only.
A program may use at most 128 MiB of HBM per device.

v0:
```python
import functools
import math

import jax
import jax.numpy as jnp
from jax import lax
from jax.experimental import pallas as pl
from jax.experimental.pallas import tpu as pltpu
from jax.sharding import PartitionSpec as P


CAP = 2
LAGS = 16
PAIRS = LAGS // 2
CSTRIDE = 2047
LANES = 128
F32 = jnp.float32
BF16 = jnp.bfloat16


def sincos(counts, period):
    half = period // 2
    signed = ((counts + half) & (period - 1)) - half
    x = signed.astype(F32) * (1.0 / period)
    u = x * x
    p = math.pi
    s = -(p**11) / 39916800.0
    for a in (p**9 / 362880.0, -(p**7) / 5040.0, p**5 / 120.0, -(p**3) / 6.0, p):
        s = s * u + a
    s = s * x
    c = p**12 / 479001600.0
    for a in (-(p**10) / 3628800.0, p**8 / 40320.0, -(p**6) / 720.0, p**4 / 24.0, -(p**2) / 2.0, 1.0):
        c = c * u + a
    return 1.0 - 2.0 * s * s, 2.0 * s * c


def dot_t(a, b):
    return lax.dot_general(a, b, (((1,), (1,)), ((), ())), preferred_element_type=F32)


def rotate(c, s, dc, ds):
    return c * dc - s * ds, s * dc + c * ds


def norm_add(acc_ref, w, load, bins):
    rows = acc_ref.shape[0]
    chunk = min(rows, 64)
    for r in range(0, rows, chunk):
        n = acc_ref[r : r + chunk, :]
        for lo in range(0, bins, LANES):
            re = load(0, r, chunk, lo).astype(F32)
            im = load(1, r, chunk, lo).astype(F32)
            n = n + (re * re + im * im) * w[:, lo : lo + LANES]
        acc_ref[r : r + chunk, :] = n


def norm_row(n):
    if n.shape[0] < LANES:
        n = jnp.concatenate([n, jnp.zeros((LANES - n.shape[0], LANES), F32)], axis=0)
    return jnp.sum(n.T, axis=0, keepdims=True)


def coarse_kernel(
    info_ref, w_ref, h_ref, *rest, blocks, segs, banks, freqs, steps, kc, period
):
    spec_refs = rest[:blocks]
    keep_ref, send_ref = rest[blocks : blocks + 2]
    a_refs, b_refs, y_refs = (rest[blocks + i : blocks + i + 2] for i in (2, 4, 6))
    acc_ref, nacc_ref, tab_ref, ctr_ref = rest[blocks + 8 :]
    step = pl.program_id(0)
    base = info_ref[0]
    bank = info_ref[1]
    freq = info_ref[2]
    total = banks * segs
    cols = total * LAGS

    def gen(which, chunk):
        a_ref, b_ref, y_ref = a_refs[which], b_refs[which], y_refs[which]
        shift = pl.multiple_of(chunk * kc, kc)
        w = w_ref[:, pl.ds(shift, kc)]
        for k in range(blocks):
            source = lax.rem(bank - k + banks, banks)
            for i in range(segs):
                a_ref[source, 2 * i : 2 * i + 2, :] = spec_refs[k][i, :, pl.ds(shift, kc)].astype(F32) * w
        odd = 2 * lax.broadcasted_iota(jnp.int32, (PAIRS, LANES), 0) + 1
        dc, ds = sincos(shift * odd * CSTRIDE, period)
        ec, es = sincos(jnp.full((PAIRS, LANES), shift * (15 * CSTRIDE), jnp.int32), period)
        for lo in range(0, kc, LANES):
            lanes = slice(lo, lo + LANES)
            c, s = rotate(ctr_ref[0, :, lanes], ctr_ref[1, :, lanes], ec, es)
            for b in range(0, total, 4):
                re, im = (
                    jnp.concatenate(
                        [a_ref[(b + i) // segs, 2 * ((b + i) % segs) + c : 2 * ((b + i) % segs) + c + 1, lanes] for i in range(4)],
                        axis=0,
                    )
                    for c in range(2)
                )
                b_ref[0, b : b + 4, lanes] = re * c[:4] - im * s[:4]
                b_ref[1, b : b + 4, lanes] = re * s[:4] + im * c[:4]
            c, s = rotate(tab_ref[0, :, lanes], tab_ref[1, :, lanes], dc, ds)
            b_ref[2, :PAIRS, lanes] = c
            b_ref[3, :PAIRS, lanes] = s
            re = b_ref[0, :, lanes]
            im = b_ref[1, :, lanes]
            for m in range(PAIRS):
                cm = b_ref[2, m : m + 1, lanes]
                sm = b_ref[3, m : m + 1, lanes]
                rc = re * cm
                js = im * sm
                jc = im * cm
                rs = re * sm
                for sign, (yr, yi) in enumerate(((rc - js, jc + rs), (rc + js, jc - rs))):
                    at = (2 * m + sign) * total
                    yr = yr.astype(BF16)
                    yi = yi.astype(BF16)
                    y_ref[at : at + total, lo : lo + LANES] = yr
                    y_ref[at : at + total, kc + lo : kc + lo + LANES] = yi
                    y_ref[cols + at : cols + at + total, lo : lo + LANES] = yi
                    y_ref[cols + at : cols + at + total, kc + lo : kc + lo + LANES] = -yr

    @pl.when(step == 0)
    def _():
        ids = base + lax.broadcasted_iota(jnp.int32, (PAIRS, kc), 1)
        odd = 2 * lax.broadcasted_iota(jnp.int32, (PAIRS, kc), 0) + 1
        c, s = sincos(ids * odd * CSTRIDE, period)
        tab_ref[0] = c
        tab_ref[1] = s
        c, s = sincos(ids * (15 * CSTRIDE), period)
        ctr_ref[0] = c
        ctr_ref[1] = s
        acc_ref[...] = jnp.zeros_like(acc_ref)
        nacc_ref[...] = jnp.zeros_like(nacc_ref)
        gen(0, step)

    for half in range(2):
        lo = half * kc
        gen(1 - half, jnp.minimum(2 * step + half + 1, 2 * steps - 1))
        h = jnp.concatenate([h_ref[0, :, lo : lo + kc], h_ref[1, :, lo : lo + kc]], axis=1)
        acc_ref[...] += dot_t(h, y_refs[half][...])
    w = w_ref[:, pl.ds(pl.multiple_of(step * 2 * kc, 2 * kc), 2 * kc)]
    norm_add(nacc_ref, w, lambda c, r, n, lo: h_ref[c, r : r + n, lo : lo + LANES], 2 * kc)

    @pl.when(step == steps - 1)
    def _():
        part = acc_ref.shape[0] // freqs
        size = min(part, LANES)

        def lay(ref, dest):
            first = pl.multiple_of(dest * part, part)
            ref[:part, :] = acc_ref[pl.ds(first, part), :]
            for r in range(0, part, size):
                row = norm_row(nacc_ref[pl.ds(first + r, size), :])
                ref[part : part + 8, r : r + LANES] = jnp.broadcast_to(row, (8, LANES))

        lay(keep_ref, freq)
        for k in range(1, freqs):
            lay(send_ref.at[k - 1], lax.rem(freq + k, freqs))


def coarse_final_kernel(keep_ref, *rest, freqs, total):
    recv_refs = rest[: freqs - 1]
    out_ref = rest[freqs - 1]
    part = keep_ref.shape[0] - 8
    cols = total * LAGS
    corr = keep_ref[...]
    for ref in recv_refs:
        corr = corr + ref[0]
    norms = corr[part : part + 1]
    cr = corr[:part, :cols]
    ci = corr[:part, cols:]
    e = cr * cr + ci * ci
    width = cols
    while width > max(total, LANES):
        width //= 2
        e = jnp.maximum(e[:, :width], e[:, width:])
    while width > total:
        width //= 2
        e = jnp.maximum(e, pltpu.roll(e, LANES - width, 1))
    size = min(part, LANES)
    for r in range(0, part, size):
        rows = e[r : r + size]
        if size < LANES:
            rows = jnp.concatenate([rows, jnp.zeros((LANES - size, LANES), F32)], axis=0)
        out = rows.T[:total] / norms[:, r : r + LANES]
        out_ref[:, r : r + size] = out[:, :size]


def ranked_pairs(trig_ref, first, segs, top, target):
    taken = jnp.int32(0)
    found = [jnp.int32(0) for _ in range(CAP)]
    for p in range(segs * top):
        hit = (trig_ref[p % top, first + p // top] == target).astype(jnp.int32)
        for c in range(CAP):
            found[c] = jnp.where(jnp.logical_and(hit == 1, taken == c), p, found[c])
        taken = taken + hit
    return taken, found


def pick_kernel(info_ref, trig_ref, off_ref, spec_ref, *rest, banks, segs, top):
    out_refs = rest[:banks]
    mult_ref, sems = rest[banks:]
    bank = info_ref[1]
    copies = []
    for k in range(banks):
        k = (k + 1) % banks
        dest = lax.rem(bank + k, banks)
        _, found = ranked_pairs(trig_ref, bank * segs, segs, top, dest)
        for c in range(CAP):
            copy = pltpu.make_async_copy(
                spec_ref.at[found[c] // top], out_refs[k].at[c], sems.at[k * CAP + c]
            )
            copy.start()
            copies.append(copy)
    line = lax.broadcasted_iota(jnp.int32, mult_ref.shape, 0)
    mult = jnp.zeros(mult_ref.shape, jnp.int32)
    for k in range(banks):
        source = lax.rem(bank - k + banks, banks)
        _, found = ranked_pairs(trig_ref, source * segs, segs, top, bank)
        for c in range(CAP):
            offset = off_ref[lax.rem(found[c], top), source * segs + found[c] // top]
            mult = jnp.where(line == k * CAP + c, 2 * offset + (LAGS - 1), mult)
    mult_ref[...] = mult
    for copy in copies:
        copy.wait()


def place_kernel(info_ref, trig_ref, *rest, banks, segs, top):
    back_refs = rest[:banks]
    out_ref, all_ref = rest[banks:]
    bank = info_ref[1]
    part = out_ref.shape[2]
    for k in range(banks):
        all_ref[CAP * k : CAP * (k + 1), :] = back_refs[k][...]
    for p in range(segs * top):
        target = trig_ref[p % top, bank * segs + p // top]
        rank = jnp.int32(0)
        for q in range(p):
            rank = rank + (trig_ref[q % top, bank * segs + q // top] == target).astype(jnp.int32)
        at = lax.rem(target - bank + banks, banks) * CAP + jnp.minimum(rank, CAP - 1)
        out_ref[p // top, p % top : p % top + 1, :] = all_ref[pl.ds(at, 1), :][:, :part]


def fine_kernel(info_ref, w_ref, mult_ref, g_ref, *rest, blocks, freqs, steps, kc, period):
    slot_refs = rest[:blocks]
    keep_ref, send_ref = rest[blocks : blocks + 2]
    a_refs, b_refs, y_refs = (rest[blocks + i : blocks + i + 2] for i in (2, 4, 6))
    acc_ref, nacc_ref, tab_ref, ctr_ref = rest[blocks + 8 :]
    step = pl.program_id(0)
    base = info_ref[0]
    freq = info_ref[2]
    n = blocks * CAP
    cols = n * LAGS
    tsub = g_ref.shape[2]

    def gen(which, chunk):
        a_ref, b_ref, y_ref = a_refs[which], b_refs[which], y_refs[which]
        shift = pl.multiple_of(chunk * kc, kc)
        w = w_ref[:, pl.ds(shift, kc)]
        for k in range(blocks):
            for i in range(CAP):
                x = slot_refs[k][i, :, pl.ds(shift, kc)].astype(F32) * w
                a_ref[0, CAP * k + i : CAP * k + i + 1, :] = x[0:1]
                a_ref[1, CAP * k + i : CAP * k + i + 1, :] = x[1:2]
        odd = 2 * lax.broadcasted_iota(jnp.int32, (PAIRS, LANES), 0) + 1
        dc, ds = sincos(shift * odd, period)
        ec, es = sincos(shift * mult_ref[...], period)
        for lo in range(0, kc, LANES):
            lanes = slice(lo, lo + LANES)
            c, s = rotate(ctr_ref[0, :, lanes], ctr_ref[1, :, lanes], ec, es)
            re = a_ref[0, :, lanes]
            im = a_ref[1, :, lanes]
            b_ref[0, :, lanes] = re * c - im * s
            b_ref[1, :, lanes] = re * s + im * c
            c, s = rotate(tab_ref[0, :, lanes], tab_ref[1, :, lanes], dc, ds)
            for i in range(n):
                re = b_ref[0, i : i + 1, lanes]
                im = b_ref[1, i : i + 1, lanes]
                rc = re * c
                js = im * s
                jc = im * c
                rs = re * s
                at = i * LAGS
                y_ref[at : at + LAGS, lanes] = jnp.concatenate([rc - js, rc + js], axis=0).astype(BF16)
                y_ref[cols + at : cols + at + LAGS, lanes] = jnp.concatenate(
                    [jc + rs, jc - rs], axis=0
                ).astype(BF16)

    @pl.when(step == 0)
    def _():
        ids = base + lax.broadcasted_iota(jnp.int32, (PAIRS, kc), 1)
        odd = 2 * lax.broadcasted_iota(jnp.int32, (PAIRS, kc), 0) + 1
        c, s = sincos(ids * odd, period)
        tab_ref[0] = c
        tab_ref[1] = s
        ids = base + lax.broadcasted_iota(jnp.int32, (n, kc), 1)
        c, s = sincos(ids * mult_ref[:, 0:1], period)
        ctr_ref[0] = c
        ctr_ref[1] = s
        acc_ref[...] = jnp.zeros_like(acc_ref)
        nacc_ref[...] = jnp.zeros_like(nacc_ref)
        gen(0, step)

    for half in range(2):
        lo = half * kc
        gen(1 - half, jnp.minimum(2 * step + half + 1, 2 * steps - 1))
        g = jnp.concatenate([g_ref[0, 0, :, lo : lo + kc], g_ref[1, 0, :, lo : lo + kc]], axis=0)
        acc_ref[...] += dot_t(y_refs[half][...], g)
    w = w_ref[:, pl.ds(pl.multiple_of(step * 2 * kc, 2 * kc), 2 * kc)]
    norm_add(nacc_ref, w, lambda c, r, n, lo: g_ref[c, 0, r : r + n, lo : lo + LANES], 2 * kc)

    @pl.when(step == steps - 1)
    def _():
        part = tsub // freqs
        acc = acc_ref[...]
        swap = pltpu.roll(acc, LANES - tsub, 1)
        corr_real = acc[:cols] + swap[cols:]
        corr_imag = acc[cols:] - swap[:cols]
        lane = lax.broadcasted_iota(jnp.int32, (1, LANES), 1)
        norms = jnp.broadcast_to(norm_row(nacc_ref[...]), (8, LANES))

        def pack(dest):
            real, imag = corr_real, pltpu.roll(corr_imag, part, 1)
            for d in range(1, freqs):
                here = dest == d
                real = jnp.where(here, pltpu.roll(corr_real, LANES - d * part, 1), real)
                moved = corr_imag if d == 1 else pltpu.roll(corr_imag, LANES - (d - 1) * part, 1)
                imag = jnp.where(here, moved, imag)
            row = norms
            for d in range(1, freqs):
                row = jnp.where(dest == d, pltpu.roll(norms, LANES - d * part, 1), row)
            return jnp.concatenate(
                [jnp.where(lane < part, real, jnp.where(lane < 2 * part, imag, 0.0)), row], axis=0
            )

        keep_ref[...] = pack(freq)
        for k in range(1, freqs):
            send_ref[k - 1] = pack(lax.rem(freq + k, freqs))


def fine_final_kernel(keep_ref, *rest, freqs, n, part):
    recv_refs = rest[: freqs - 1]
    out_refs = rest[freqs - 1 :]
    x = keep_ref[...]
    for ref in recv_refs:
        x = x + ref[0]
    norm = x[n * LAGS : n * LAGS + 1]
    e = x[: n * LAGS]
    e = e * e
    e = e + pltpu.roll(e, LANES - part, 1)
    for i in range(n):
        top = jnp.max(e[i * LAGS : (i + 1) * LAGS], axis=0, keepdims=True)
        out_refs[i // CAP][i % CAP : i % CAP + 1, :] = top / norm


def params(mib=50, **kw):
    return pltpu.CompilerParams(vmem_limit_bytes=mib * 1024 * 1024, **kw)


SMEM = pl.BlockSpec(memory_space=pltpu.SMEM)
VMEM = pl.BlockSpec(memory_space=pltpu.VMEM)


def coarse_section(info, weight, templates, blocks, banks, freqs, period):
    segs = blocks[0].shape[0]
    rows, bins = templates.shape[1], templates.shape[2]
    total = banks * segs
    cols = total * LAGS
    kc = min(1024, bins // 2)
    steps = bins // (2 * kc)
    part = rows // freqs
    kernel = functools.partial(
        coarse_kernel, blocks=len(blocks), segs=segs, banks=banks, freqs=freqs, steps=steps, kc=kc, period=period
    )
    return pl.pallas_call(
        kernel,
        grid=(steps,),
        in_specs=[
            SMEM,
            VMEM,
            pl.BlockSpec((2, rows, 2 * kc), lambda i: (0, 0, i)),
        ]
        + [VMEM for _ in blocks],
        out_specs=[
            pl.BlockSpec((part + 8, 2 * cols), lambda i: (0, 0)),
            pl.BlockSpec((freqs - 1, part + 8, 2 * cols), lambda i: (0, 0, 0)),
        ],
        out_shape=[
            jax.ShapeDtypeStruct((part + 8, 2 * cols), F32),
            jax.ShapeDtypeStruct((freqs - 1, part + 8, 2 * cols), F32),
        ],
        scratch_shapes=[
            *[pltpu.VMEM((banks, 2 * segs, kc), F32) for _ in range(2)],
            *[pltpu.VMEM((4, total, kc), F32) for _ in range(2)],
            *[pltpu.VMEM((2 * cols, 2 * kc), BF16) for _ in range(2)],
            pltpu.VMEM((rows, 2 * cols), F32),
            pltpu.VMEM((rows, LANES), F32),
            pltpu.VMEM((2, PAIRS, kc), F32),
            pltpu.VMEM((2, PAIRS, kc), F32),
        ],
        compiler_params=params(dimension_semantics=("arbitrary",)),
        cost_estimate=pl.CostEstimate(
            flops=8 * rows * bins * cols, bytes_accessed=4 * rows * bins, transcendentals=0
        ),
        name="coarse",
    )(info, weight, templates, *blocks)


def fine_section(info, weight, mult, templates, blocks, freqs, period):
    bins = templates.shape[3]
    tsub = templates.shape[2]
    n = CAP * len(blocks)
    cols = n * LAGS
    kc = min(2048, bins // 2)
    steps = bins // (2 * kc)
    kernel = functools.partial(
        fine_kernel, blocks=len(blocks), freqs=freqs, steps=steps, kc=kc, period=period
    )
    return pl.pallas_call(
        kernel,
        grid=(steps,),
        in_specs=[
            SMEM,
            VMEM,
            VMEM,
            pl.BlockSpec((2, 1, tsub, 2 * kc), lambda i: (0, 0, 0, i)),
        ]
        + [VMEM for _ in blocks],
        out_specs=[
            pl.BlockSpec((cols + 8, LANES), lambda i: (0, 0)),
            pl.BlockSpec((freqs - 1, cols + 8, LANES), lambda i: (0, 0, 0)),
        ],
        out_shape=[
            jax.ShapeDtypeStruct((cols + 8, LANES), F32),
            jax.ShapeDtypeStruct((freqs - 1, cols + 8, LANES), F32),
        ],
        scratch_shapes=[
            *[pltpu.VMEM((2, n, kc), F32) for _ in range(4)],
            *[pltpu.VMEM((2 * cols, kc), BF16) for _ in range(2)],
            pltpu.VMEM((2 * cols, LANES), F32),
            pltpu.VMEM((tsub, LANES), F32),
            pltpu.VMEM((2, PAIRS, kc), F32),
            pltpu.VMEM((2, n, kc), F32),
        ],
        compiler_params=params(dimension_semantics=("arbitrary",)),
        cost_estimate=pl.CostEstimate(
            flops=8 * tsub * bins * cols, bytes_accessed=4 * tsub * bins, transcendentals=0
        ),
        name="fine",
    )(info, weight, mult, templates, *blocks)


def after(value, *others):
    return lax.optimization_barrier((value, *others))[0]


def shift_permute(value, axis, count, by):
    return lax.ppermute(value, axis, [(i, (i + by) % count) for i in range(count)])


def body(
    coarse_spectra,
    fine_spectra,
    coarse_templates,
    fine_templates,
    coarse_weight,
    fine_weight,
    triggers,
    offsets,
):
    banks = lax.axis_size("bank")
    freqs = lax.axis_size("freq")
    bank = lax.axis_index("bank")
    freq = lax.axis_index("freq")
    segs = fine_spectra.shape[0]
    coarse_bins = coarse_spectra.shape[2]
    fine_bins = fine_spectra.shape[2]
    top = triggers.shape[1]
    tsub = fine_templates.shape[2]
    part = tsub // freqs
    coarse_period = 4 * coarse_bins * freqs
    fine_period = 4 * fine_bins * freqs
    zero = jnp.zeros((), jnp.int32)
    coarse_info = jnp.stack([freq * coarse_bins, bank, freq, zero]).astype(jnp.int32)
    fine_info = jnp.stack([freq * fine_bins, bank, freq, zero]).astype(jnp.int32)
    coarse_weight = coarse_weight.reshape(1, -1)
    fine_weight = fine_weight.reshape(1, -1)

    coarse_blocks = [coarse_spectra] + [
        shift_permute(coarse_spectra, "bank", banks, k) for k in range(1, banks)
    ]

    *picked, mult = pl.pallas_call(
        functools.partial(pick_kernel, banks=banks, segs=segs, top=top),
        in_specs=[SMEM, SMEM, SMEM, pl.BlockSpec(memory_space=pltpu.HBM)],
        out_shape=[jax.ShapeDtypeStruct((CAP, 2, fine_bins), BF16) for _ in range(banks)]
        + [jax.ShapeDtypeStruct((banks * CAP, LANES), jnp.int32)],
        scratch_shapes=[pltpu.SemaphoreType.DMA((banks * CAP,))],
        compiler_params=params(),
        name="pick",
    )(fine_info, triggers.T, offsets.T, fine_spectra)
    order = sorted(range(banks), key=lambda k: min(k, banks - k))
    fine_blocks = {}
    for k in order:
        fine_blocks[k] = picked[k] if k == 0 else shift_permute(picked[k], "bank", banks, k)

    def exchange(send):
        return [shift_permute(send[k - 1 : k], "freq", freqs, k) for k in range(1, freqs)]

    keep, send = coarse_section(
        coarse_info, coarse_weight, coarse_templates, coarse_blocks, banks, freqs, coarse_period
    )
    coarse_keep, coarse_received = keep, exchange(send)
    done = [keep]
    back = {}
    for members in (order[:-1], order[-1:]):
        keep, send = fine_section(
            after(fine_info, *done),
            fine_weight,
            jnp.concatenate([mult[CAP * k : CAP * (k + 1)] for k in members], axis=0),
            fine_templates,
            [fine_blocks[k] for k in members],
            freqs,
            fine_period,
        )
        received = exchange(send)
        done = pl.pallas_call(
            functools.partial(fine_final_kernel, freqs=freqs, n=CAP * len(members), part=part),
            out_shape=[jax.ShapeDtypeStruct((CAP, LANES), F32) for _ in members],
            compiler_params=params(8),
            name="fine_final",
        )(keep, *received)
        for k, result in zip(members, done):
            back[k] = result if k == 0 else shift_permute(result, "bank", banks, banks - k)
    coarse_snr = pl.pallas_call(
        functools.partial(coarse_final_kernel, freqs=freqs, total=banks * segs),
        out_shape=jax.ShapeDtypeStruct((banks * segs, coarse_keep.shape[0] - 8), F32),
        compiler_params=params(16),
        name="coarse_final",
    )(after(coarse_keep, keep), *coarse_received).T
    fine_snr = pl.pallas_call(
        functools.partial(place_kernel, banks=banks, segs=segs, top=top),
        in_specs=[SMEM, SMEM] + [pl.BlockSpec(memory_space=pltpu.VMEM) for _ in range(banks)],
        out_shape=jax.ShapeDtypeStruct((segs, top, part), F32),
        scratch_shapes=[pltpu.VMEM((banks * CAP, LANES), F32)],
        compiler_params=params(8),
        name="place",
    )(fine_info, triggers.T, *[back[k] for k in range(banks)])
    return (coarse_snr, fine_snr)


def solution(mesh):
    return sharded(mesh)


def sharded(mesh):
    return jax.shard_map(
        body,
        mesh=mesh,
        in_specs=(
            P(("groups", "seg", "bank"), None, "freq"),
            P(("groups", "seg", "bank"), None, "freq"),
            P(None, "bank", "freq"),
            P(None, "bank", None, "freq"),
            P(("groups", "freq")),
            P(("groups", "freq")),
            P(("groups", "seg"), None),
            P(("groups", "seg"), None),
        ),
        out_specs=(
            P(("bank", "freq"), ("groups", "seg")),
            P(("groups", "seg", "bank"), None, "freq"),
        ),
        check_vma=False,
    )
```

profile of v0, /device:TPU:0, one launch (start us, length us, event | category | flops | bytes accessed | tf_op | source)
XLA Modules:
  0.0 76.2 jit_solution(4225845793365178623)
XLA Ops:
  0.6 4.1 %collective-permute-start.1 = (bf16[4,2,8192]{2,1,0:T(2,128)(2,1)}, bf16[4,2,8192]{2,1,0:T(2,128)(2,1)S(1)}, u32[]{:S(2)}, u32[]{:S(2)}) collective-permute-start(bf16[4,2,8192]{2,1,0:T(2,128)(2,1)} %rest_0_.1), channel_id=1, source_target_pairs={{0,8},{4,12},{8,0},{12,4},{1,9},{5,13},{9,1},{13,5},{2,10},{6,14},... | collective-permute-start | bytes 393224 | tf_op jit(solution)/shard_map/ppermute | solution.py:458
  4.8 1.6 %collective-permute-start = (bf16[4,2,8192]{2,1,0:T(2,128)(2,1)}, bf16[4,2,8192]{2,1,0:T(2,128)(2,1)S(1)}, u32[]{:S(2)}, u32[]{:S(2)}) collective-permute-start(bf16[4,2,8192]{2,1,0:T(2,128)(2,1)} %rest_0_.1), channel_id=1, source_target_pairs={{0,4},{4,8},{8,12},{12,0},{1,5},{5,9},{9,13},{13,1},{2,6},{6,10},{... | collective-permute-start | bytes 393224 | tf_op jit(solution)/shard_map/ppermute | solution.py:458
  6.3 2.2 %collective-permute-start.2 = (bf16[4,2,8192]{2,1,0:T(2,128)(2,1)}, bf16[4,2,8192]{2,1,0:T(2,128)(2,1)S(1)}, u32[]{:S(2)}, u32[]{:S(2)}) collective-permute-start(bf16[4,2,8192]{2,1,0:T(2,128)(2,1)} %rest_0_.1), channel_id=1, source_target_pairs={{0,12},{4,0},{8,4},{12,8},{1,13},{5,1},{9,5},{13,9},{2,14},{6,2},{... | collective-permute-start | bytes 393224 | tf_op jit(solution)/shard_map/ppermute | solution.py:458
  8.7 1.0 %copy-done.1 = bf16[4,2,32768]{2,1,0:T(2,128)(2,1)S(1)} copy-done((bf16[4,2,32768]{2,1,0:T(2,128)(2,1)S(1)}, bf16[4,2,32768]{2,1,0:T(2,128)(2,1)}, u32[]{:S(2)}) %copy-start.1) | copy-done | bytes 524312
  9.7 0.7 copy-done.2
  10.4 0.7 copy-done.4
  11.1 2.3 %pick.1 = (bf16[2,2,32768]{2,1,0:T(2,128)(2,1)S(1)}, bf16[2,2,32768]{2,1,0:T(2,128)(2,1)S(1)}, bf16[2,2,32768]{2,1,0:T(2,128)(2,1)S(1)}, bf16[2,2,32768]{2,1,0:T(2,128)(2,1)S(1)}, s32[8,128]{1,0:T(8,128)S(1)}) custom-call(s32[4]{0:T(128)S(1)} %pad_add_fusion.1.info_ref, s32[2,16]{1,0:T(2,128)S(1)} %bitcast.11, s32[2,16]{1,0:T(2,128)S(1)} %bitcast.13, ...), custom_call_target="tpu_custom_call" | custom-call | tf_op jit(solution)/shard_map/pick/pallas_call | solution.py:493
  13.4 3.8 %collective-permute-start.4 = (bf16[2,2,32768]{2,1,0:T(2,128)(2,1)S(1)}, bf16[2,2,32768]{2,1,0:T(2,128)(2,1)S(1)}, u32[]{:S(2)}, u32[]{:S(2)}) collective-permute-start(bf16[2,2,32768]{2,1,0:T(2,128)(2,1)S(1)} %get-tuple-element.24), channel_id=1, source_target_pairs={{0,12},{4,0},{8,4},{12,8},{1,13},{5,1},{9,5},{13,9},{2,14},{6,2},{... | collective-permute-start | bytes 786440 | tf_op jit(solution)/shard_map/ppermute | solution.py:458
  17.4 0.9 %copy-done.5 = bf16[4,2,8192]{2,1,0:T(2,128)(2,1)S(1)} copy-done((bf16[4,2,8192]{2,1,0:T(2,128)(2,1)S(1)}, bf16[4,2,8192]{2,1,0:T(2,128)(2,1)}, u32[]{:S(2)}) %copy-start.5) | copy-done | bytes 131096
  18.3 0.8 copy-done.6
  19.0 17.9 %coarse.1 = (f32[264,512]{1,0:T(8,128)S(1)}, f32[1,264,512]{2,1,0:T(8,128)S(1)}) custom-call(s32[4]{0:T(128)S(1)} %pad_add_fusion.2.info_ref, f32[1,8192]{1,0:T(1,128)S(1)} %bitcast.14, bf16[2,512,8192]{2,1,0:T(8,128)(2,1)} %h_ref.1, bf16[4,2,8192]{2,1,0:T(2,128)(2,1)S(1)} %copy-done.5, bf16[4,2,8192]{2,1,0:T(2,128)(2,1)S(1)} %collective-permute-done.rest_1_, ...), custom_call_target="tpu_custom_call" | custom-call | flops 8589934592 | bytes 16777216 | tf_op jit(solution)/shard_map/coarse/pallas_call | solution.py:375
  37.0 1.6 %collective-permute-start.7 = (f32[1,264,512]{2,1,0:T(8,128)S(1)}, f32[1,264,512]{2,1,0:T(8,128)S(1)}, u32[]{:S(2)}, u32[]{:S(2)}) collective-permute-start(f32[1,264,512]{2,1,0:T(8,128)S(1)} %get-tuple-element.34), channel_id=1, source_target_pairs={{0,2},{2,0},{1,3},{3,1},{4,6},{6,4},{5,7},{7,5},{8,10},{10,8},{9,1... | collective-permute-start | bytes 1622024 | tf_op jit(solution)/shard_map/ppermute | solution.py:458
  38.6 11.1 %fine.2 = (f32[104,128]{1,0:T(8,128)S(1)}, f32[1,104,128]{2,1,0:T(8,128)S(1)}) custom-call(s32[4]{0:T(128)S(1)} %pad_add_fusion.1.info_ref, f32[1,32768]{1,0:T(1,128)S(1)} %bitcast.9, s32[6,128]{1,0:T(8,128)S(1)} %pad_add_fusion.mult_ref, bf16[2,1,64,32768]{3,2,1,0:T(8,128)(2,1)} %g_ref.3, bf16[2,2,32768]{2,1,0:T(2,128)(2,1)S(1)} %get-tuple-element.22.rest_0_, ...), custom_call_target="tpu_custom_call" | custom-call | flops 1610612736 | bytes 8388608 | tf_op jit(solution)/shard_map/fine/pallas_call | solution.py:419
  49.6 0.6 collective-permute-start.5
  50.2 3.6 %collective-permute-done.5.rest_0_ = f32[1,104,128]{2,1,0:T(8,128)S(1)} collective-permute-done((f32[1,104,128]{2,1,0:T(8,128)S(1)}, f32[1,104,128]{2,1,0:T(8,128)S(1)}, u32[]{:S(2)}, u32[]{:S(2)}) %collective-permute-start.5) | collective-permute-done | bytes 53280 | tf_op jit(solution)/shard_map/ppermute | solution.py:458
  53.8 0.1 fine_final.2
  53.9 9.0 %fine.3 = (f32[40,128]{1,0:T(8,128)S(1)}, f32[1,40,128]{2,1,0:T(8,128)S(1)}) custom-call(s32[4]{0:T(128)S(1)} %pad_add_fusion.1.info_ref, f32[1,32768]{1,0:T(1,128)S(1)} %bitcast.10, s32[2,128]{1,0:T(2,128)S(1)} %get-tuple-element.36.mult_ref, bf16[2,1,64,32768]{3,2,1,0:T(8,128)(2,1)} %g_ref.3, bf16[2,2,32768]{2,1,0:T(2,128)(2,1)S(1)} %collective-permute-done.6.rest_0_), custom_call_target="tpu_custom_call" | custom-call | flops 536870912 | bytes 8388608 | tf_op jit(solution)/shard_map/fine/pallas_call | solution.py:419
  63.0 0.6 collective-permute-start.9
  63.6 0.9 %collective-permute-start.8 = (f32[2,128]{1,0:T(2,128)S(1)}, f32[2,128]{1,0:T(2,128)S(1)}, u32[]{:S(2)}, u32[]{:S(2)}) collective-permute-start(f32[2,128]{1,0:T(2,128)S(1)} %get-tuple-element.28), channel_id=1, source_target_pairs={{0,12},{4,0},{8,4},{12,8},{1,13},{5,1},{9,5},{13,9},{2,14},{6,2},{... | collective-permute-start | bytes 3080 | tf_op jit(solution)/shard_map/ppermute | solution.py:458
  64.5 5.0 %collective-permute-start.11 = (f32[2,128]{1,0:T(2,128)S(1)}, f32[2,128]{1,0:T(2,128)S(1)}, u32[]{:S(2)}, u32[]{:S(2)}) collective-permute-start(f32[2,128]{1,0:T(2,128)S(1)} %get-tuple-element.29), channel_id=1, source_target_pairs={{0,4},{4,8},{8,12},{12,0},{1,5},{5,9},{9,13},{13,1},{2,6},{6,10},{... | collective-permute-start | bytes 3080 | tf_op jit(solution)/shard_map/ppermute | solution.py:458
  69.5 2.3 %collective-permute-start.10 = (f32[2,128]{1,0:T(2,128)S(1)}, f32[2,128]{1,0:T(2,128)S(1)}, u32[]{:S(2)}, u32[]{:S(2)}) collective-permute-start(f32[2,128]{1,0:T(2,128)S(1)} %fine_final.3), channel_id=1, source_target_pairs={{0,8},{4,12},{8,0},{12,4},{1,9},{5,13},{9,1},{13,5},{2,10},{6,14},... | collective-permute-start | bytes 3080 | tf_op jit(solution)/shard_map/ppermute | solution.py:458
  71.8 2.2 %collective-permute-done.10.rest_2_ = f32[2,128]{1,0:T(2,128)S(1)} collective-permute-done((f32[2,128]{1,0:T(2,128)S(1)}, f32[2,128]{1,0:T(2,128)S(1)}, u32[]{:S(2)}, u32[]{:S(2)}) %collective-permute-start.10) | collective-permute-done | bytes 1056 | tf_op jit(solution)/shard_map/ppermute | solution.py:458
  74.0 1.2 %place.1 = f32[4,2,32]{2,1,0:T(2,128)} custom-call(s32[4]{0:T(128)S(1)} %pad_add_fusion.1.info_ref, s32[2,16]{1,0:T(2,128)S(1)} %bitcast.12, f32[2,128]{1,0:T(2,128)S(1)} %get-tuple-element.27.rest_0_, f32[2,128]{1,0:T(2,128)S(1)} %collective-permute-done.8.rest_1_, f32[2,128]{1,0:T(2,128)S(1)} %collective-permute-done.10.rest_2_, ...), custom_call_target="tpu_custom_call" | custom-call | tf_op jit(solution)/shard_map/place/pallas_call | solution.py:541
  75.3 0.9 %coarse_final.1 = f32[16,256]{1,0:T(8,128)} custom-call(f32[264,512]{1,0:T(8,128)S(1)} %get-tuple-element.33.keep_ref, f32[1,264,512]{2,1,0:T(8,128)S(1)} %collective-permute-done.7.rest_0_), custom_call_target="tpu_custom_call" | custom-call | tf_op jit(solution)/shard_map/coarse_final/pallas_call | solution.py:535
  (27 shorter events, 0.4 us)
Async XLA Ops:
  0.6 37.9 %copy-start = (f32[32768]{0:T(1024)S(1)}, f32[32768]{0:T(1024)}, u32[]{:S(2)}) copy-start(f32[32768]{0:T(1024)} %param.13) | copy-start | bytes 393220
  0.6 16.7 %collective-permute-start.1 = (bf16[4,2,8192]{2,1,0:T(2,128)(2,1)}, bf16[4,2,8192]{2,1,0:T(2,128)(2,1)S(1)}, u32[]{:S(2)}, u32[]{:S(2)}) collective-permute-start(bf16[4,2,8192]{2,1,0:T(2,128)(2,1)} %rest_0_.1), channel_id=1, source_target_pairs={{0,8},{4,12},{8,0},{12,4},{1,9},{5,13},{9,1},{13,5},{2,10},{6,14},... | collective-permute-start | bytes 393224 | tf_op jit(solution)/shard_map/ppermute | solution.py:458
  4.8 12.6 %collective-permute-start = (bf16[4,2,8192]{2,1,0:T(2,128)(2,1)}, bf16[4,2,8192]{2,1,0:T(2,128)(2,1)S(1)}, u32[]{:S(2)}, u32[]{:S(2)}) collective-permute-start(bf16[4,2,8192]{2,1,0:T(2,128)(2,1)} %rest_0_.1), channel_id=1, source_target_pairs={{0,4},{4,8},{8,12},{12,0},{1,5},{5,9},{9,13},{13,1},{2,6},{6,10},{... | collective-permute-start | bytes 393224 | tf_op jit(solution)/shard_map/ppermute | solution.py:458
  6.3 11.0 %collective-permute-start.2 = (bf16[4,2,8192]{2,1,0:T(2,128)(2,1)}, bf16[4,2,8192]{2,1,0:T(2,128)(2,1)S(1)}, u32[]{:S(2)}, u32[]{:S(2)}) collective-permute-start(bf16[4,2,8192]{2,1,0:T(2,128)(2,1)} %rest_0_.1), channel_id=1, source_target_pairs={{0,12},{4,0},{8,4},{12,8},{1,13},{5,1},{9,5},{13,9},{2,14},{6,2},{... | collective-permute-start | bytes 393224 | tf_op jit(solution)/shard_map/ppermute | solution.py:458
  8.7 1.0 %copy-start.1 = (bf16[4,2,32768]{2,1,0:T(2,128)(2,1)S(1)}, bf16[4,2,32768]{2,1,0:T(2,128)(2,1)}, u32[]{:S(2)}) copy-start(bf16[4,2,32768]{2,1,0:T(2,128)(2,1)} %spec_ref.1) | copy-start | bytes 1572868
  9.7 0.7 copy-start.2
  10.4 0.7 copy-start.4
  13.4 25.2 %collective-permute-start.3 = (bf16[2,2,32768]{2,1,0:T(2,128)(2,1)S(1)}, bf16[2,2,32768]{2,1,0:T(2,128)(2,1)S(1)}, u32[]{:S(2)}, u32[]{:S(2)}) collective-permute-start(bf16[2,2,32768]{2,1,0:T(2,128)(2,1)S(1)} %get-tuple-element.23), channel_id=1, source_target_pairs={{0,4},{4,8},{8,12},{12,0},{1,5},{5,9},{9,13},{13,1},{2,6},{6,10},{... | collective-permute-start | bytes 786440 | tf_op jit(solution)/shard_map/ppermute | solution.py:458
  13.4 25.1 %collective-permute-start.4 = (bf16[2,2,32768]{2,1,0:T(2,128)(2,1)S(1)}, bf16[2,2,32768]{2,1,0:T(2,128)(2,1)S(1)}, u32[]{:S(2)}, u32[]{:S(2)}) collective-permute-start(bf16[2,2,32768]{2,1,0:T(2,128)(2,1)S(1)} %get-tuple-element.24), channel_id=1, source_target_pairs={{0,12},{4,0},{8,4},{12,8},{1,13},{5,1},{9,5},{13,9},{2,14},{6,2},{... | collective-permute-start | bytes 786440 | tf_op jit(solution)/shard_map/ppermute | solution.py:458
  17.3 36.6 %collective-permute-start.6 = (bf16[2,2,32768]{2,1,0:T(2,128)(2,1)S(1)}, bf16[2,2,32768]{2,1,0:T(2,128)(2,1)S(1)}, u32[]{:S(2)}, u32[]{:S(2)}) collective-permute-start(bf16[2,2,32768]{2,1,0:T(2,128)(2,1)S(1)} %get-tuple-element.31), channel_id=1, source_target_pairs={{0,8},{4,12},{8,0},{12,4},{1,9},{5,13},{9,1},{13,5},{2,10},{6,14},... | collective-permute-start | bytes 786440 | tf_op jit(solution)/shard_map/ppermute | solution.py:458
  17.4 0.9 %copy-start.5 = (bf16[4,2,8192]{2,1,0:T(2,128)(2,1)S(1)}, bf16[4,2,8192]{2,1,0:T(2,128)(2,1)}, u32[]{:S(2)}) copy-start(bf16[4,2,8192]{2,1,0:T(2,128)(2,1)} %rest_0_.1) | copy-start | bytes 393220
  18.3 0.8 copy-start.6
  36.9 37.1 %copy-start.3 = (s32[16,2]{0,1:T(2,128)S(1)}, s32[16,2]{0,1:T(2,128)}, u32[]{:S(2)}) copy-start(s32[16,2]{0,1:T(2,128)} %param.14) | copy-start | bytes 388
  37.0 38.3 %collective-permute-start.7 = (f32[1,264,512]{2,1,0:T(8,128)S(1)}, f32[1,264,512]{2,1,0:T(8,128)S(1)}, u32[]{:S(2)}, u32[]{:S(2)}) collective-permute-start(f32[1,264,512]{2,1,0:T(8,128)S(1)} %get-tuple-element.34), channel_id=1, source_target_pairs={{0,2},{2,0},{1,3},{3,1},{4,6},{6,4},{5,7},{7,5},{8,10},{10,8},{9,1... | collective-permute-start | bytes 1622024 | tf_op jit(solution)/shard_map/ppermute | solution.py:458
  49.6 4.2 %collective-permute-start.5 = (f32[1,104,128]{2,1,0:T(8,128)S(1)}, f32[1,104,128]{2,1,0:T(8,128)S(1)}, u32[]{:S(2)}, u32[]{:S(2)}) collective-permute-start(f32[1,104,128]{2,1,0:T(8,128)S(1)} %get-tuple-element.26), channel_id=1, source_target_pairs={{0,2},{2,0},{1,3},{3,1},{4,6},{6,4},{5,7},{7,5},{8,10},{10,8},{9,1... | collective-permute-start | bytes 159752 | tf_op jit(solution)/shard_map/ppermute | solution.py:458
  63.0 6.5 %collective-permute-start.9 = (f32[1,40,128]{2,1,0:T(8,128)S(1)}, f32[1,40,128]{2,1,0:T(8,128)S(1)}, u32[]{:S(2)}, u32[]{:S(2)}) collective-permute-start(f32[1,40,128]{2,1,0:T(8,128)S(1)} %get-tuple-element.35), channel_id=1, source_target_pairs={{0,2},{2,0},{1,3},{3,1},{4,6},{6,4},{5,7},{7,5},{8,10},{10,8},{9,1... | collective-permute-start | bytes 61448 | tf_op jit(solution)/shard_map/ppermute | solution.py:458
  63.6 8.2 %collective-permute-start.8 = (f32[2,128]{1,0:T(2,128)S(1)}, f32[2,128]{1,0:T(2,128)S(1)}, u32[]{:S(2)}, u32[]{:S(2)}) collective-permute-start(f32[2,128]{1,0:T(2,128)S(1)} %get-tuple-element.28), channel_id=1, source_target_pairs={{0,12},{4,0},{8,4},{12,8},{1,13},{5,1},{9,5},{13,9},{2,14},{6,2},{... | collective-permute-start | bytes 3080 | tf_op jit(solution)/shard_map/ppermute | solution.py:458
  64.5 7.3 %collective-permute-start.11 = (f32[2,128]{1,0:T(2,128)S(1)}, f32[2,128]{1,0:T(2,128)S(1)}, u32[]{:S(2)}, u32[]{:S(2)}) collective-permute-start(f32[2,128]{1,0:T(2,128)S(1)} %get-tuple-element.29), channel_id=1, source_target_pairs={{0,4},{4,8},{8,12},{12,0},{1,5},{5,9},{9,13},{13,1},{2,6},{6,10},{... | collective-permute-start | bytes 3080 | tf_op jit(solution)/shard_map/ppermute | solution.py:458
  69.5 4.5 %collective-permute-start.10 = (f32[2,128]{1,0:T(2,128)S(1)}, f32[2,128]{1,0:T(2,128)S(1)}, u32[]{:S(2)}, u32[]{:S(2)}) collective-permute-start(f32[2,128]{1,0:T(2,128)S(1)} %fine_final.3), channel_id=1, source_target_pairs={{0,8},{4,12},{8,0},{12,4},{1,9},{5,13},{9,1},{13,5},{2,10},{6,14},... | collective-permute-start | bytes 3080 | tf_op jit(solution)/shard_map/ppermute | solution.py:458
where the time goes:
time: 77.4 us; the launch traced here: 76.2 us
  Pallas kernels  42.6 us (55%)
  starting transfers between devices  22.7 us (29%)
  waiting for transfers between devices  5.87 us (8%)
  local copies, waits for them, and re-layouts  4.07 us (5%)
    ppermute x12, starting transfers between devices, shift_permute(): lax.ppermute(value, axis, [(i, (i + by) % count) for i in range(count)])  22.7 us
    pallas_call x2, Pallas kernels, fine_section(): pl.pallas_call(kernel, grid=(steps,), in_specs=[SMEM, VMEM, VMEM, pl.Bloc...  20.1 us
    pallas_call x1, Pallas kernels, coarse_section(): pl.pallas_call(kernel, grid=(steps,), in_specs=[SMEM, VMEM, pl.BlockSpec(...  17.9 us
    ppermute x12, waiting for transfers between devices, shift_permute(): lax.ppermute(value, axis, [(i, (i + by) % count) for i in range(count)])  5.87 us
    unnamed x14, local copies, waits for them, and re-layouts  4.07 us
    pallas_call x1, Pallas kernels, body(): pl.pallas_call(functools.partial(pick_kernel, banks=banks, segs=segs, top...  2.29 us
  transfers between devices with their start and end apart: 12, of which 2 were waited for; matrix products, arithmetic and copies ran while one was open for 0% of the time, Pallas kernels for 55%

commit v1 on v0

--- a/solution.py
+++ b/solution.py
@@ -61,18 +61,24 @@
 
 
 def coarse_kernel(
-    info_ref, w_ref, h_ref, *rest, blocks, segs, banks, freqs, steps, kc, period
+    info_ref, w_ref, h_ref, *rest, blocks, segs, banks, freqs, chunks, kc, period
 ):
     spec_refs = rest[:blocks]
     keep_ref, send_ref = rest[blocks : blocks + 2]
     a_refs, b_refs, y_refs = (rest[blocks + i : blocks + i + 2] for i in (2, 4, 6))
-    acc_ref, nacc_ref, tab_ref, ctr_ref = rest[blocks + 8 :]
-    step = pl.program_id(0)
+    acc_ref, nacc_ref, tab_ref, ctr_ref, held_ref, sems = rest[blocks + 8 :]
     base = info_ref[0]
     bank = info_ref[1]
     freq = info_ref[2]
     total = banks * segs
     cols = total * LAGS
+
+    def fetch(chunk):
+        at = pl.ds(pl.multiple_of(chunk * kc, kc), kc)
+        return pltpu.make_async_copy(h_ref.at[:, :, at], held_ref.at[chunk], sems.at[chunk])
+
+    for chunk in range(chunks):
+        fetch(chunk).start()
 
     def gen(which, chunk):
         a_ref, b_ref, y_ref = a_refs[which], b_refs[which], y_refs[which]
@@ -119,43 +125,44 @@
                     y_ref[cols + at : cols + at + total, lo : lo + LANES] = yi
                     y_ref[cols + at : cols + at + total, kc + lo : kc + lo + LANES] = -yr
 
-    @pl.when(step == 0)
-    def _():
-        ids = base + lax.broadcasted_iota(jnp.int32, (PAIRS, kc), 1)
-        odd = 2 * lax.broadcasted_iota(jnp.int32, (PAIRS, kc), 0) + 1
-        c, s = sincos(ids * odd * CSTRIDE, period)
-        tab_ref[0] = c
-        tab_ref[1] = s
-        c, s = sincos(ids * (15 * CSTRIDE), period)
-        ctr_ref[0] = c
-        ctr_ref[1] = s
-        acc_ref[...] = jnp.zeros_like(acc_ref)
-        nacc_ref[...] = jnp.zeros_like(nacc_ref)
-        gen(0, step)
-
-    for half in range(2):
-        lo = half * kc
-        gen(1 - half, jnp.minimum(2 * step + half + 1, 2 * steps - 1))
-        h = jnp.concatenate([h_ref[0, :, lo : lo + kc], h_ref[1, :, lo : lo + kc]], axis=1)
-        acc_ref[...] += dot_t(h, y_refs[half][...])
-    w = w_ref[:, pl.ds(pl.multiple_of(step * 2 * kc, 2 * kc), 2 * kc)]
-    norm_add(nacc_ref, w, lambda c, r, n, lo: h_ref[c, r : r + n, lo : lo + LANES], 2 * kc)
-
-    @pl.when(step == steps - 1)
-    def _():
-        part = acc_ref.shape[0] // freqs
-        size = min(part, LANES)
-
-        def lay(ref, dest):
-            first = pl.multiple_of(dest * part, part)
-            ref[:part, :] = acc_ref[pl.ds(first, part), :]
-            for r in range(0, part, size):
-                row = norm_row(nacc_ref[pl.ds(first + r, size), :])
-                ref[part : part + 8, r : r + LANES] = jnp.broadcast_to(row, (8, LANES))
-
-        lay(keep_ref, freq)
-        for k in range(1, freqs):
-            lay(send_ref.at[k - 1], lax.rem(freq + k, freqs))
+    ids = base + lax.broadcasted_iota(jnp.int32, (PAIRS, kc), 1)
+    odd = 2 * lax.broadcasted_iota(jnp.int32, (PAIRS, kc), 0) + 1
+    c, s = sincos(ids * odd * CSTRIDE, period)
+    tab_ref[0] = c
+    tab_ref[1] = s
+    c, s = sincos(ids * (15 * CSTRIDE), period)
+    ctr_ref[0] = c
+    ctr_ref[1] = s
+    acc_ref[...] = jnp.zeros_like(acc_ref)
+    nacc_ref[...] = jnp.zeros_like(nacc_ref)
+    gen(0, jnp.int32(0))
+
+    def pair(turn, carry):
+        fetch(2 * turn).wait()
+        fetch(2 * turn + 1).wait()
+        for half in range(2):
+            chunk = 2 * turn + half
+            gen(1 - half, jnp.minimum(chunk + 1, chunks - 1))
+            w = w_ref[:, pl.ds(pl.multiple_of(chunk * kc, kc), kc)]
+            norm_add(nacc_ref, w, lambda c, r, n, at: held_ref[chunk, c, r : r + n, at : at + LANES], kc)
+            h = jnp.concatenate([held_ref[chunk, 0], held_ref[chunk, 1]], axis=1)
+            acc_ref[...] += dot_t(h, y_refs[half][...])
+        return carry
+
+    lax.fori_loop(0, chunks // 2, pair, 0)
+    part = acc_ref.shape[0] // freqs
+    size = min(part, LANES)
+
+    def lay(ref, dest):
+        first = pl.multiple_of(dest * part, part)
+        ref[:part, :] = acc_ref[pl.ds(first, part), :]
+        for r in range(0, part, size):
+            row = norm_row(nacc_ref[pl.ds(first + r, size), :])
+            ref[part : part + 8, r : r + LANES] = jnp.broadcast_to(row, (8, LANES))
+
+    lay(keep_ref, freq)
+    for k in range(1, freqs):
+        lay(send_ref.at[k - 1], lax.rem(freq + k, freqs))
 
 
 def coarse_final_kernel(keep_ref, *rest, freqs, total):
@@ -241,17 +248,23 @@
         out_ref[p // top, p % top : p % top + 1, :] = all_ref[pl.ds(at, 1), :][:, :part]
 
 
-def fine_kernel(info_ref, w_ref, mult_ref, g_ref, *rest, blocks, freqs, steps, kc, period):
+def fine_kernel(info_ref, w_ref, mult_ref, g_ref, *rest, blocks, freqs, chunks, kc, period):
     slot_refs = rest[:blocks]
     keep_ref, send_ref = rest[blocks : blocks + 2]
     a_refs, b_refs, y_refs = (rest[blocks + i : blocks + i + 2] for i in (2, 4, 6))
-    acc_ref, nacc_ref, tab_ref, ctr_ref = rest[blocks + 8 :]
-    step = pl.program_id(0)
+    acc_ref, nacc_ref, tab_ref, ctr_ref, held_ref, sems = rest[blocks + 8 :]
     base = info_ref[0]
     freq = info_ref[2]
     n = blocks * CAP
     cols = n * LAGS
     tsub = g_ref.shape[2]
+
+    def fetch(chunk):
+        at = pl.ds(pl.multiple_of(chunk * kc, kc), kc)
+        return pltpu.make_async_copy(g_ref.at[:, 0, :, at], held_ref.at[chunk], sems.at[chunk])
+
+    for chunk in range(chunks):
+        fetch(chunk).start()
 
     def gen(which, chunk):
         a_ref, b_ref, y_ref = a_refs[which], b_refs[which], y_refs[which]
@@ -286,56 +299,57 @@
                     [jc + rs, jc - rs], axis=0
                 ).astype(BF16)
 
-    @pl.when(step == 0)
-    def _():
-        ids = base + lax.broadcasted_iota(jnp.int32, (PAIRS, kc), 1)
-        odd = 2 * lax.broadcasted_iota(jnp.int32, (PAIRS, kc), 0) + 1
-        c, s = sincos(ids * odd, period)
-        tab_ref[0] = c
-        tab_ref[1] = s
-        ids = base + lax.broadcasted_iota(jnp.int32, (n, kc), 1)
-        c, s = sincos(ids * mult_ref[:, 0:1], period)
-        ctr_ref[0] = c
-        ctr_ref[1] = s
-        acc_ref[...] = jnp.zeros_like(acc_ref)
-        nacc_ref[...] = jnp.zeros_like(nacc_ref)
-        gen(0, step)
-
-    for half in range(2):
-        lo = half * kc
-        gen(1 - half, jnp.minimum(2 * step + half + 1, 2 * steps - 1))
-        g = jnp.concatenate([g_ref[0, 0, :, lo : lo + kc], g_ref[1, 0, :, lo : lo + kc]], axis=0)
-        acc_ref[...] += dot_t(y_refs[half][...], g)
-    w = w_ref[:, pl.ds(pl.multiple_of(step * 2 * kc, 2 * kc), 2 * kc)]
-    norm_add(nacc_ref, w, lambda c, r, n, lo: g_ref[c, 0, r : r + n, lo : lo + LANES], 2 * kc)
-
-    @pl.when(step == steps - 1)
-    def _():
-        part = tsub // freqs
-        acc = acc_ref[...]
-        swap = pltpu.roll(acc, LANES - tsub, 1)
-        corr_real = acc[:cols] + swap[cols:]
-        corr_imag = acc[cols:] - swap[:cols]
-        lane = lax.broadcasted_iota(jnp.int32, (1, LANES), 1)
-        norms = jnp.broadcast_to(norm_row(nacc_ref[...]), (8, LANES))
-
-        def pack(dest):
-            real, imag = corr_real, pltpu.roll(corr_imag, part, 1)
-            for d in range(1, freqs):
-                here = dest == d
-                real = jnp.where(here, pltpu.roll(corr_real, LANES - d * part, 1), real)
-                moved = corr_imag if d == 1 else pltpu.roll(corr_imag, LANES - (d - 1) * part, 1)
-                imag = jnp.where(here, moved, imag)
-            row = norms
-            for d in range(1, freqs):
-                row = jnp.where(dest == d, pltpu.roll(norms, LANES - d * part, 1), row)
-            return jnp.concatenate(
-                [jnp.where(lane < part, real, jnp.where(lane < 2 * part, imag, 0.0)), row], axis=0
-            )
-
-        keep_ref[...] = pack(freq)
-        for k in range(1, freqs):
-            send_ref[k - 1] = pack(lax.rem(freq + k, freqs))
+    ids = base + lax.broadcasted_iota(jnp.int32, (PAIRS, kc), 1)
+    odd = 2 * lax.broadcasted_iota(jnp.int32, (PAIRS, kc), 0) + 1
+    c, s = sincos(ids * odd, period)
+    tab_ref[0] = c
+    tab_ref[1] = s
+    ids = base + lax.broadcasted_iota(jnp.int32, (n, kc), 1)
+    c, s = sincos(ids * mult_ref[:, 0:1], period)
+    ctr_ref[0] = c
+    ctr_ref[1] = s
+    acc_ref[...] = jnp.zeros_like(acc_ref)
+    nacc_ref[...] = jnp.zeros_like(nacc_ref)
+    gen(0, jnp.int32(0))
+
+    def pair(turn, carry):
+        fetch(2 * turn).wait()
+        fetch(2 * turn + 1).wait()
+        for half in range(2):
+            chunk = 2 * turn + half
+            gen(1 - half, jnp.minimum(chunk + 1, chunks - 1))
+            w = w_ref[:, pl.ds(pl.multiple_of(chunk * kc, kc), kc)]
+            norm_add(nacc_ref, w, lambda c, r, n, at: held_ref[chunk, c, r : r + n, at : at + LANES], kc)
+            g = jnp.concatenate([held_ref[chunk, 0], held_ref[chunk, 1]], axis=0)
+            acc_ref[...] += dot_t(y_refs[half][...], g)
+        return carry
+
+    lax.fori_loop(0, chunks // 2, pair, 0)
+    part = tsub // freqs
+    acc = acc_ref[...]
+    swap = pltpu.roll(acc, LANES - tsub, 1)
+    corr_real = acc[:cols] + swap[cols:]
+    corr_imag = acc[cols:] - swap[:cols]
+    lane = lax.broadcasted_iota(jnp.int32, (1, LANES), 1)
+    norms = jnp.broadcast_to(norm_row(nacc_ref[...]), (8, LANES))
+
+    def pack(dest):
+        real, imag = corr_real, pltpu.roll(corr_imag, part, 1)
+        for d in range(1, freqs):
+            here = dest == d
+            real = jnp.where(here, pltpu.roll(corr_real, LANES - d * part, 1), real)
+            moved = corr_imag if d == 1 else pltpu.roll(corr_imag, LANES - (d - 1) * part, 1)
+            imag = jnp.where(here, moved, imag)
+        row = norms
+        for d in range(1, freqs):
+            row = jnp.where(dest == d, pltpu.roll(norms, LANES - d * part, 1), row)
+        return jnp.concatenate(
+            [jnp.where(lane < part, real, jnp.where(lane < 2 * part, imag, 0.0)), row], axis=0
+        )
+
+    keep_ref[...] = pack(freq)
+    for k in range(1, freqs):
+        send_ref[k - 1] = pack(lax.rem(freq + k, freqs))
 
 
 def fine_final_kernel(keep_ref, *rest, freqs, n, part):
@@ -359,6 +373,7 @@
 
 SMEM = pl.BlockSpec(memory_space=pltpu.SMEM)
 VMEM = pl.BlockSpec(memory_space=pltpu.VMEM)
+HBM = pl.BlockSpec(memory_space=pltpu.HBM)
 
 
 def coarse_section(info, weight, templates, blocks, banks, freqs, period):
@@ -367,24 +382,19 @@
     total = banks * segs
     cols = total * LAGS
     kc = min(1024, bins // 2)
-    steps = bins // (2 * kc)
+    chunks = bins // kc
     part = rows // freqs
     kernel = functools.partial(
-        coarse_kernel, blocks=len(blocks), segs=segs, banks=banks, freqs=freqs, steps=steps, kc=kc, period=period
+        coarse_kernel, blocks=len(blocks), segs=segs, banks=banks, freqs=freqs, chunks=chunks, kc=kc, period=period
     )
     return pl.pallas_call(
         kernel,
-        grid=(steps,),
         in_specs=[
             SMEM,
             VMEM,
-            pl.BlockSpec((2, rows, 2 * kc), lambda i: (0, 0, i)),
+            HBM,
         ]
         + [VMEM for _ in blocks],
-        out_specs=[
-            pl.BlockSpec((part + 8, 2 * cols), lambda i: (0, 0)),
-            pl.BlockSpec((freqs - 1, part + 8, 2 * cols), lambda i: (0, 0, 0)),
-        ],
         out_shape=[
             jax.ShapeDtypeStruct((part + 8, 2 * cols), F32),
             jax.ShapeDtypeStruct((freqs - 1, part + 8, 2 * cols), F32),
@@ -397,8 +407,10 @@
             pltpu.VMEM((rows, LANES), F32),
             pltpu.VMEM((2, PAIRS, kc), F32),
             pltpu.VMEM((2, PAIRS, kc), F32),
+            pltpu.VMEM((chunks, 2, rows, kc), BF16),
+            pltpu.SemaphoreType.DMA((chunks,)),
         ],
-        compiler_params=params(dimension_semantics=("arbitrary",)),
+        compiler_params=params(),
         cost_estimate=pl.CostEstimate(
             flops=8 * rows * bins * cols, bytes_accessed=4 * rows * bins, transcendentals=0
         ),
@@ -411,25 +423,20 @@
     tsub = templates.shape[2]
     n = CAP * len(blocks)
     cols = n * LAGS
-    kc = min(2048, bins // 2)
-    steps = bins // (2 * kc)
+    kc = min(4096, bins // 2)
+    chunks = bins // kc
     kernel = functools.partial(
-        fine_kernel, blocks=len(blocks), freqs=freqs, steps=steps, kc=kc, period=period
+        fine_kernel, blocks=len(blocks), freqs=freqs, chunks=chunks, kc=kc, period=period
     )
     return pl.pallas_call(
         kernel,
-        grid=(steps,),
         in_specs=[
             SMEM,
             VMEM,
             VMEM,
-            pl.BlockSpec((2, 1, tsub, 2 * kc), lambda i: (0, 0, 0, i)),
+            HBM,
         ]
         + [VMEM for _ in blocks],
-        out_specs=[
-            pl.BlockSpec((cols + 8, LANES), lambda i: (0, 0)),
-            pl.BlockSpec((freqs - 1, cols + 8, LANES), lambda i: (0, 0, 0)),
-        ],
         out_shape=[
             jax.ShapeDtypeStruct((cols + 8, LANES), F32),
             jax.ShapeDtypeStruct((freqs - 1, cols + 8, LANES), F32),
@@ -441,8 +448,10 @@
             pltpu.VMEM((tsub, LANES), F32),
             pltpu.VMEM((2, PAIRS, kc), F32),
             pltpu.VMEM((2, n, kc), F32),
+            pltpu.VMEM((chunks, 2, tsub, kc), BF16),
+            pltpu.SemaphoreType.DMA((chunks,)),
         ],
-        compiler_params=params(dimension_semantics=("arbitrary",)),
+        compiler_params=params(),
         cost_estimate=pl.CostEstimate(
             flops=8 * tsub * bins * cols, bytes_accessed=4 * tsub * bins, transcendentals=0
         ),
@@ -511,33 +520,32 @@
         coarse_info, coarse_weight, coarse_templates, coarse_blocks, banks, freqs, coarse_period
     )
     coarse_keep, coarse_received = keep, exchange(send)
-    done = [keep]
-    back = {}
-    for members in (order[:-1], order[-1:]):
-        keep, send = fine_section(
-            after(fine_info, *done),
-            fine_weight,
-            jnp.concatenate([mult[CAP * k : CAP * (k + 1)] for k in members], axis=0),
-            fine_templates,
-            [fine_blocks[k] for k in members],
-            freqs,
-            fine_period,
-        )
-        received = exchange(send)
-        done = pl.pallas_call(
-            functools.partial(fine_final_kernel, freqs=freqs, n=CAP * len(members), part=part),
-            out_shape=[jax.ShapeDtypeStruct((CAP, LANES), F32) for _ in members],
-            compiler_params=params(8),
-            name="fine_final",
-        )(keep, *received)
-        for k, result in zip(members, done):
-            back[k] = result if k == 0 else shift_permute(result, "bank", banks, banks - k)
+    keep, send = fine_section(
+        after(fine_info, coarse_keep),
+        fine_weight,
+        mult,
+        fine_templates,
+        [fine_blocks[k] for k in range(banks)],
+        freqs,
+        fine_period,
+    )
+    received = exchange(send)
     coarse_snr = pl.pallas_call(
         functools.partial(coarse_final_kernel, freqs=freqs, total=banks * segs),
         out_shape=jax.ShapeDtypeStruct((banks * segs, coarse_keep.shape[0] - 8), F32),
         compiler_params=params(16),
         name="coarse_final",
-    )(after(coarse_keep, keep), *coarse_received).T
+    )(after(coarse_keep, keep), *coarse_received)
+    results = pl.pallas_call(
+        functools.partial(fine_final_kernel, freqs=freqs, n=CAP * banks, part=part),
+        out_shape=[jax.ShapeDtypeStruct((CAP, LANES), F32) for _ in range(banks)],
+        compiler_params=params(8),
+        name="fine_final",
+    )(after(keep, coarse_snr), *received)
+    back = [
+        results[k] if k == 0 else shift_permute(results[k], "bank", banks, banks - k)
+        for k in range(banks)
+    ]
     fine_snr = pl.pallas_call(
         functools.partial(place_kernel, banks=banks, segs=segs, top=top),
         in_specs=[SMEM, SMEM] + [pl.BlockSpec(memory_space=pltpu.VMEM) for _ in range(banks)],
@@ -545,8 +553,8 @@
         scratch_shapes=[pltpu.VMEM((banks * CAP, LANES), F32)],
         compiler_params=params(8),
         name="place",
-    )(fine_info, triggers.T, *[back[k] for k in range(banks)])
-    return (coarse_snr, fine_snr)
+    )(fine_info, triggers.T, *back)
+    return (coarse_snr.T, fine_snr)
 
 
 def solution(mesh):

time: 77.4 us -> 92.5 us (1.20); the launches traced: 76.2 us -> 92.3 us
  waiting for transfers between devices: 5.87 us -> 27.1 us
  Pallas kernels: 42.6 us -> 34.7 us
  starting transfers between devices: 22.7 us -> 27.9 us
  local copies, waits for them, and re-layouts: 4.07 us -> 1.68 us
    ppermute x12 -> x11, waiting for transfers between devices: 5.87 us -> 27.1 us  [shift_permute(): lax.ppermute(value, axis, [(i, (i + by) % count) for i in range(count)])]
    pallas_call x3 -> x2, Pallas kernels: 38 us -> 30.2 us  [the longest x1 17.8 us: coarse_section(): pl.pallas_call(kernel, in_specs=[SMEM, VMEM, HBM] + [VMEM for _ in blocks...]
    ppermute x12 -> x11, starting transfers between devices: 22.7 us -> 27.9 us  [shift_permute(): lax.ppermute(value, axis, [(i, (i + by) % count) for i in range(count)])]
    unnamed x14 -> x12, local copies, waits for them, and re-layouts: 4.07 us -> 1.68 us
  transfers between devices with their start and end apart: 12 -> 11, of which waited for: 2 -> 8; matrix products, arithmetic and copies ran while one was open for 0% -> 0% of each run, Pallas kernels for 55% -> 17%
where the time goes in v1:
time: 92.5 us; the launch traced here: 92.3 us
  Pallas kernels  34.7 us (38%)
  starting transfers between devices  27.9 us (30%)
  waiting for transfers between devices  27.1 us (29%)
  local copies, waits for them, and re-layouts  1.68 us (2%)
    ppermute x11, starting transfers between devices, shift_permute(): lax.ppermute(value, axis, [(i, (i + by) % count) for i in range(count)])  27.9 us
    ppermute x11, waiting for transfers between devices, shift_permute(): lax.ppermute(value, axis, [(i, (i + by) % count) for i in range(count)])  27.1 us
    pallas_call x1, Pallas kernels, coarse_section(): pl.pallas_call(kernel, in_specs=[SMEM, VMEM, HBM] + [VMEM for _ in blocks...  17.8 us
    pallas_call x1, Pallas kernels, fine_section(): pl.pallas_call(kernel, in_specs=[SMEM, VMEM, VMEM, HBM] + [VMEM for _ in...  12.4 us
    pallas_call x1, Pallas kernels, body(): pl.pallas_call(functools.partial(pick_kernel, banks=banks, segs=segs, top...  2.3 us
  transfers between devices with their start and end apart: 11, of which 8 were waited for; matrix products, arithmetic and copies ran while one was open for 0% of the time, Pallas kernels for 17%

profile of v1, /device:TPU:0, one launch (start us, length us, event | category | flops | bytes accessed | tf_op | source)
XLA Modules:
  0.0 92.3 jit_solution(14151357672639246643)
XLA Ops:
  0.7 4.1 %collective-permute-start.1 = (bf16[4,2,8192]{2,1,0:T(2,128)(2,1)}, bf16[4,2,8192]{2,1,0:T(2,128)(2,1)S(1)}, u32[]{:S(2)}, u32[]{:S(2)}) collective-permute-start(bf16[4,2,8192]{2,1,0:T(2,128)(2,1)} %rest_0_.1), channel_id=1, source_target_pairs={{0,8},{4,12},{8,0},{12,4},{1,9},{5,13},{9,1},{13,5},{2,10},{6,14},... | collective-permute-start | bytes 393224 | tf_op jit(solution)/shard_map/ppermute | solution.py:467
  4.8 1.6 %collective-permute-start = (bf16[4,2,8192]{2,1,0:T(2,128)(2,1)}, bf16[4,2,8192]{2,1,0:T(2,128)(2,1)S(1)}, u32[]{:S(2)}, u32[]{:S(2)}) collective-permute-start(bf16[4,2,8192]{2,1,0:T(2,128)(2,1)} %rest_0_.1), channel_id=1, source_target_pairs={{0,4},{4,8},{8,12},{12,0},{1,5},{5,9},{9,13},{13,1},{2,6},{6,10},{... | collective-permute-start | bytes 393224 | tf_op jit(solution)/shard_map/ppermute | solution.py:467
  6.4 2.2 %collective-permute-start.2 = (bf16[4,2,8192]{2,1,0:T(2,128)(2,1)}, bf16[4,2,8192]{2,1,0:T(2,128)(2,1)S(1)}, u32[]{:S(2)}, u32[]{:S(2)}) collective-permute-start(bf16[4,2,8192]{2,1,0:T(2,128)(2,1)} %rest_0_.1), channel_id=1, source_target_pairs={{0,12},{4,0},{8,4},{12,8},{1,13},{5,1},{9,5},{13,9},{2,14},{6,2},{... | collective-permute-start | bytes 393224 | tf_op jit(solution)/shard_map/ppermute | solution.py:467
  8.7 6.3 %collective-permute-done.1.rest_2_ = bf16[4,2,8192]{2,1,0:T(2,128)(2,1)S(1)} collective-permute-done((bf16[4,2,8192]{2,1,0:T(2,128)(2,1)}, bf16[4,2,8192]{2,1,0:T(2,128)(2,1)S(1)}, u32[]{:S(2)}, u32[]{:S(2)}) %collective-permute-start.1) | collective-permute-done | bytes 131104 | tf_op jit(solution)/shard_map/ppermute | solution.py:467
  15.0 0.7 collective-permute-done.2.rest_3_
  15.7 0.9 copy-done.4
  16.6 0.8 copy-done.5
  17.4 17.8 %coarse.1 = (f32[264,512]{1,0:T(8,128)S(1)}, f32[1,264,512]{2,1,0:T(8,128)S(1)}) custom-call(s32[4]{0:T(128)S(1)} %pad_add_fusion.1.info_ref, f32[1,8192]{1,0:T(1,128)S(1)} %bitcast.13, bf16[2,512,8192]{2,1,0:T(8,128)(2,1)} %h_ref.1, bf16[4,2,8192]{2,1,0:T(2,128)(2,1)S(1)} %copy-done.4, bf16[4,2,8192]{2,1,0:T(2,128)(2,1)S(1)} %collective-permute-done.rest_1_, ...), custom_call_target="tpu_custom_call" | custom-call | flops 8589934592 | bytes 16777216 | tf_op jit(solution)/shard_map/coarse/pallas_call | solution.py:390
  35.2 1.6 %collective-permute-start.6 = (f32[1,264,512]{2,1,0:T(8,128)S(1)}, f32[1,264,512]{2,1,0:T(8,128)S(1)}, u32[]{:S(2)}, u32[]{:S(2)}) collective-permute-start(f32[1,264,512]{2,1,0:T(8,128)S(1)} %get-tuple-element.27), channel_id=1, source_target_pairs={{0,2},{2,0},{1,3},{3,1},{4,6},{6,4},{5,7},{7,5},{8,10},{10,8},{9,1... | collective-permute-start | bytes 1622024 | tf_op jit(solution)/shard_map/ppermute | solution.py:467
  36.9 2.3 %pick.1 = (bf16[2,2,32768]{2,1,0:T(2,128)(2,1)S(1)}, bf16[2,2,32768]{2,1,0:T(2,128)(2,1)S(1)}, bf16[2,2,32768]{2,1,0:T(2,128)(2,1)S(1)}, bf16[2,2,32768]{2,1,0:T(2,128)(2,1)S(1)}, s32[8,128]{1,0:T(8,128)S(1)}) custom-call(s32[4]{0:T(128)S(1)} %pad_add_fusion.info_ref, s32[2,16]{1,0:T(2,128)S(1)} %bitcast.10, s32[2,16]{1,0:T(2,128)S(1)} %bitcast.12, ...), custom_call_target="tpu_custom_call" | custom-call | tf_op jit(solution)/shard_map/pick/pallas_call | solution.py:502
  39.2 2.1 %collective-permute-start.3 = (bf16[2,2,32768]{2,1,0:T(2,128)(2,1)S(1)}, bf16[2,2,32768]{2,1,0:T(2,128)(2,1)S(1)}, u32[]{:S(2)}, u32[]{:S(2)}) collective-permute-start(bf16[2,2,32768]{2,1,0:T(2,128)(2,1)S(1)} %get-tuple-element.22), channel_id=1, source_target_pairs={{0,4},{4,8},{8,12},{12,0},{1,5},{5,9},{9,13},{13,1},{2,6},{6,10},{... | collective-permute-start | bytes 786440 | tf_op jit(solution)/shard_map/ppermute | solution.py:467
  41.2 1.9 %collective-permute-start.4 = (bf16[2,2,32768]{2,1,0:T(2,128)(2,1)S(1)}, bf16[2,2,32768]{2,1,0:T(2,128)(2,1)S(1)}, u32[]{:S(2)}, u32[]{:S(2)}) collective-permute-start(bf16[2,2,32768]{2,1,0:T(2,128)(2,1)S(1)} %get-tuple-element.23), channel_id=1, source_target_pairs={{0,8},{4,12},{8,0},{12,4},{1,9},{5,13},{9,1},{13,5},{2,10},{6,14},... | collective-permute-start | bytes 786440 | tf_op jit(solution)/shard_map/ppermute | solution.py:467
  43.1 2.8 %collective-permute-start.5 = (bf16[2,2,32768]{2,1,0:T(2,128)(2,1)S(1)}, bf16[2,2,32768]{2,1,0:T(2,128)(2,1)S(1)}, u32[]{:S(2)}, u32[]{:S(2)}) collective-permute-start(bf16[2,2,32768]{2,1,0:T(2,128)(2,1)S(1)} %get-tuple-element.24), channel_id=1, source_target_pairs={{0,12},{4,0},{8,4},{12,8},{1,13},{5,1},{9,5},{13,9},{2,14},{6,2},{... | collective-permute-start | bytes 786440 | tf_op jit(solution)/shard_map/ppermute | solution.py:467
  46.0 2.8 %collective-permute-done.3.rest_1_ = bf16[2,2,32768]{2,1,0:T(2,128)(2,1)S(1)} collective-permute-done((bf16[2,2,32768]{2,1,0:T(2,128)(2,1)S(1)}, bf16[2,2,32768]{2,1,0:T(2,128)(2,1)S(1)}, u32[]{:S(2)}, u32[]{:S(2)}) %collective-permute-start.3) | collective-permute-done | bytes 262176 | tf_op jit(solution)/shard_map/ppermute | solution.py:467
  48.8 9.8 %collective-permute-done.4.rest_2_ = bf16[2,2,32768]{2,1,0:T(2,128)(2,1)S(1)} collective-permute-done((bf16[2,2,32768]{2,1,0:T(2,128)(2,1)S(1)}, bf16[2,2,32768]{2,1,0:T(2,128)(2,1)S(1)}, u32[]{:S(2)}, u32[]{:S(2)}) %collective-permute-start.4) | collective-permute-done | bytes 262176 | tf_op jit(solution)/shard_map/ppermute | solution.py:467
  58.6 12.4 %fine.1 = (f32[136,128]{1,0:T(8,128)S(1)}, f32[1,136,128]{2,1,0:T(8,128)S(1)}) custom-call(s32[4]{0:T(128)S(1)} %pad_add_fusion.info_ref, f32[1,32768]{1,0:T(1,128)S(1)} %bitcast.9, s32[8,128]{1,0:T(8,128)S(1)} %get-tuple-element.20.mult_ref, bf16[2,1,64,32768]{3,2,1,0:T(8,128)(2,1)} %g_ref.1, bf16[2,2,32768]{2,1,0:T(2,128)(2,1)S(1)} %get-tuple-element.21.rest_0_, ...), custom_call_target="tpu_custom_call" | custom-call | flops 2147483648 | bytes 8388608 | tf_op jit(solution)/shard_map/fine/pallas_call | solution.py:431
  71.0 0.8 collective-permute-start.7
  71.8 0.9 coarse_final.1
  72.7 2.7 %collective-permute-done.7.rest_0_ = f32[1,136,128]{2,1,0:T(8,128)S(1)} collective-permute-done((f32[1,136,128]{2,1,0:T(8,128)S(1)}, f32[1,136,128]{2,1,0:T(8,128)S(1)}, u32[]{:S(2)}, u32[]{:S(2)}) %collective-permute-start.7) | collective-permute-done | bytes 69664 | tf_op jit(solution)/shard_map/ppermute | solution.py:467
  75.5 10.2 %collective-permute-start.8 = (f32[2,128]{1,0:T(2,128)S(1)}, f32[2,128]{1,0:T(2,128)S(1)}, u32[]{:S(2)}, u32[]{:S(2)}) collective-permute-start(f32[2,128]{1,0:T(2,128)S(1)} %get-tuple-element.31), channel_id=1, source_target_pairs={{0,12},{4,0},{8,4},{12,8},{1,13},{5,1},{9,5},{13,9},{2,14},{6,2},{... | collective-permute-start | bytes 3080 | tf_op jit(solution)/shard_map/ppermute | solution.py:467
  86.3 0.7 collective-permute-done.8.rest_1_
  87.0 3.2 %collective-permute-done.9.rest_2_ = f32[2,128]{1,0:T(2,128)S(1)} collective-permute-done((f32[2,128]{1,0:T(2,128)S(1)}, f32[2,128]{1,0:T(2,128)S(1)}, u32[]{:S(2)}, u32[]{:S(2)}) %collective-permute-start.9) | collective-permute-done | bytes 1056 | tf_op jit(solution)/shard_map/ppermute | solution.py:467
  90.1 0.9 collective-permute-done.10.rest_3_
  91.0 1.2 %place.1 = f32[4,2,32]{2,1,0:T(2,128)} custom-call(s32[4]{0:T(128)S(1)} %pad_add_fusion.info_ref, s32[2,16]{1,0:T(2,128)S(1)} %bitcast.11, f32[2,128]{1,0:T(2,128)S(1)} %get-tuple-element.30.rest_0_, f32[2,128]{1,0:T(2,128)S(1)} %collective-permute-done.8.rest_1_, f32[2,128]{1,0:T(2,128)S(1)} %collective-permute-done.9.rest_2_, ...), custom_call_target="tpu_custom_call" | custom-call | tf_op jit(solution)/shard_map/place/pallas_call | solution.py:549
  (18 shorter events, 0.9 us)
Async XLA Ops:
  0.6 36.2 %copy-start.3 = (s32[16,2]{0,1:T(2,128)S(1)}, s32[16,2]{0,1:T(2,128)}, u32[]{:S(2)}) copy-start(s32[16,2]{0,1:T(2,128)} %param.15) | copy-start | bytes 388
  0.6 36.2 %copy-start.2 = (s32[16,2]{0,1:T(2,128)S(1)}, s32[16,2]{0,1:T(2,128)}, u32[]{:S(2)}) copy-start(s32[16,2]{0,1:T(2,128)} %param.14) | copy-start | bytes 388
  0.7 36.2 %copy-start = (bf16[4,2,32768]{2,1,0:T(2,128)(2,1)S(1)}, bf16[4,2,32768]{2,1,0:T(2,128)(2,1)}, u32[]{:S(2)}) copy-start(bf16[4,2,32768]{2,1,0:T(2,128)(2,1)} %spec_ref.1) | copy-start | bytes 1572868
  0.7 58.0 %copy-start.1 = (f32[32768]{0:T(1024)S(1)}, f32[32768]{0:T(1024)}, u32[]{:S(2)}) copy-start(f32[32768]{0:T(1024)} %param.13) | copy-start | bytes 393220
  0.7 14.4 %collective-permute-start.1 = (bf16[4,2,8192]{2,1,0:T(2,128)(2,1)}, bf16[4,2,8192]{2,1,0:T(2,128)(2,1)S(1)}, u32[]{:S(2)}, u32[]{:S(2)}) collective-permute-start(bf16[4,2,8192]{2,1,0:T(2,128)(2,1)} %rest_0_.1), channel_id=1, source_target_pairs={{0,8},{4,12},{8,0},{12,4},{1,9},{5,13},{9,1},{13,5},{2,10},{6,14},... | collective-permute-start | bytes 393224 | tf_op jit(solution)/shard_map/ppermute | solution.py:467
  4.8 10.2 %collective-permute-start = (bf16[4,2,8192]{2,1,0:T(2,128)(2,1)}, bf16[4,2,8192]{2,1,0:T(2,128)(2,1)S(1)}, u32[]{:S(2)}, u32[]{:S(2)}) collective-permute-start(bf16[4,2,8192]{2,1,0:T(2,128)(2,1)} %rest_0_.1), channel_id=1, source_target_pairs={{0,4},{4,8},{8,12},{12,0},{1,5},{5,9},{9,13},{13,1},{2,6},{6,10},{... | collective-permute-start | bytes 393224 | tf_op jit(solution)/shard_map/ppermute | solution.py:467
  6.4 9.3 %collective-permute-start.2 = (bf16[4,2,8192]{2,1,0:T(2,128)(2,1)}, bf16[4,2,8192]{2,1,0:T(2,128)(2,1)S(1)}, u32[]{:S(2)}, u32[]{:S(2)}) collective-permute-start(bf16[4,2,8192]{2,1,0:T(2,128)(2,1)} %rest_0_.1), channel_id=1, source_target_pairs={{0,12},{4,0},{8,4},{12,8},{1,13},{5,1},{9,5},{13,9},{2,14},{6,2},{... | collective-permute-start | bytes 393224 | tf_op jit(solution)/shard_map/ppermute | solution.py:467
  15.7 0.9 copy-start.4
  16.6 0.8 copy-start.5
  35.2 36.6 %collective-permute-start.6 = (f32[1,264,512]{2,1,0:T(8,128)S(1)}, f32[1,264,512]{2,1,0:T(8,128)S(1)}, u32[]{:S(2)}, u32[]{:S(2)}) collective-permute-start(f32[1,264,512]{2,1,0:T(8,128)S(1)} %get-tuple-element.27), channel_id=1, source_target_pairs={{0,2},{2,0},{1,3},{3,1},{4,6},{6,4},{5,7},{7,5},{8,10},{10,8},{9,1... | collective-permute-start | bytes 1622024 | tf_op jit(solution)/shard_map/ppermute | solution.py:467
  39.2 9.6 %collective-permute-start.3 = (bf16[2,2,32768]{2,1,0:T(2,128)(2,1)S(1)}, bf16[2,2,32768]{2,1,0:T(2,128)(2,1)S(1)}, u32[]{:S(2)}, u32[]{:S(2)}) collective-permute-start(bf16[2,2,32768]{2,1,0:T(2,128)(2,1)S(1)} %get-tuple-element.22), channel_id=1, source_target_pairs={{0,4},{4,8},{8,12},{12,0},{1,5},{5,9},{9,13},{13,1},{2,6},{6,10},{... | collective-permute-start | bytes 786440 | tf_op jit(solution)/shard_map/ppermute | solution.py:467
  41.2 17.4 %collective-permute-start.4 = (bf16[2,2,32768]{2,1,0:T(2,128)(2,1)S(1)}, bf16[2,2,32768]{2,1,0:T(2,128)(2,1)S(1)}, u32[]{:S(2)}, u32[]{:S(2)}) collective-permute-start(bf16[2,2,32768]{2,1,0:T(2,128)(2,1)S(1)} %get-tuple-element.23), channel_id=1, source_target_pairs={{0,8},{4,12},{8,0},{12,4},{1,9},{5,13},{9,1},{13,5},{2,10},{6,14},... | collective-permute-start | bytes 786440 | tf_op jit(solution)/shard_map/ppermute | solution.py:467
  43.1 15.5 %collective-permute-start.5 = (bf16[2,2,32768]{2,1,0:T(2,128)(2,1)S(1)}, bf16[2,2,32768]{2,1,0:T(2,128)(2,1)S(1)}, u32[]{:S(2)}, u32[]{:S(2)}) collective-permute-start(bf16[2,2,32768]{2,1,0:T(2,128)(2,1)S(1)} %get-tuple-element.24), channel_id=1, source_target_pairs={{0,12},{4,0},{8,4},{12,8},{1,13},{5,1},{9,5},{13,9},{2,14},{6,2},{... | collective-permute-start | bytes 786440 | tf_op jit(solution)/shard_map/ppermute | solution.py:467
  71.0 4.4 %collective-permute-start.7 = (f32[1,136,128]{2,1,0:T(8,128)S(1)}, f32[1,136,128]{2,1,0:T(8,128)S(1)}, u32[]{:S(2)}, u32[]{:S(2)}) collective-permute-start(f32[1,136,128]{2,1,0:T(8,128)S(1)} %get-tuple-element.29), channel_id=1, source_target_pairs={{0,2},{2,0},{1,3},{3,1},{4,6},{6,4},{5,7},{7,5},{8,10},{10,8},{9,1... | collective-permute-start | bytes 208904 | tf_op jit(solution)/shard_map/ppermute | solution.py:467
  75.5 11.5 %collective-permute-start.8 = (f32[2,128]{1,0:T(2,128)S(1)}, f32[2,128]{1,0:T(2,128)S(1)}, u32[]{:S(2)}, u32[]{:S(2)}) collective-permute-start(f32[2,128]{1,0:T(2,128)S(1)} %get-tuple-element.31), channel_id=1, source_target_pairs={{0,12},{4,0},{8,4},{12,8},{1,13},{5,1},{9,5},{13,9},{2,14},{6,2},{... | collective-permute-start | bytes 3080 | tf_op jit(solution)/shard_map/ppermute | solution.py:467
  85.7 4.5 %collective-permute-start.9 = (f32[2,128]{1,0:T(2,128)S(1)}, f32[2,128]{1,0:T(2,128)S(1)}, u32[]{:S(2)}, u32[]{:S(2)}) collective-permute-start(f32[2,128]{1,0:T(2,128)S(1)} %get-tuple-element.32), channel_id=1, source_target_pairs={{0,8},{4,12},{8,0},{12,4},{1,9},{5,13},{9,1},{13,5},{2,10},{6,14},... | collective-permute-start | bytes 3080 | tf_op jit(solution)/shard_map/ppermute | solution.py:467
  85.7 5.4 %collective-permute-start.10 = (f32[2,128]{1,0:T(2,128)S(1)}, f32[2,128]{1,0:T(2,128)S(1)}, u32[]{:S(2)}, u32[]{:S(2)}) collective-permute-start(f32[2,128]{1,0:T(2,128)S(1)} %get-tuple-element.33), channel_id=1, source_target_pairs={{0,4},{4,8},{8,12},{12,0},{1,5},{5,9},{9,13},{13,1},{2,6},{6,10},{... | collective-permute-start | bytes 3080 | tf_op jit(solution)/shard_map/ppermute | solution.py:467

commit v2 on v1

--- a/solution.py
+++ b/solution.py
@@ -42,16 +42,20 @@
     return c * dc - s * ds, s * dc + c * ds
 
 
-def norm_add(acc_ref, w, load, bins):
+def norm_add(acc_ref, w_ref, held_ref, chunk, turn, turns):
     rows = acc_ref.shape[0]
-    chunk = min(rows, 64)
-    for r in range(0, rows, chunk):
-        n = acc_ref[r : r + chunk, :]
-        for lo in range(0, bins, LANES):
-            re = load(0, r, chunk, lo).astype(F32)
-            im = load(1, r, chunk, lo).astype(F32)
-            n = n + (re * re + im * im) * w[:, lo : lo + LANES]
-        acc_ref[r : r + chunk, :] = n
+    bins = held_ref.shape[3]
+    count = max(rows // turns, 16)
+    r = turn * count
+    if r >= rows:
+        return
+    n = acc_ref[r : r + count, :]
+    for lo in range(0, bins, LANES):
+        re = held_ref[chunk, 0, r : r + count, lo : lo + LANES].astype(F32)
+        im = held_ref[chunk, 1, r : r + count, lo : lo + LANES].astype(F32)
+        w = w_ref[:, pl.ds(pl.multiple_of(chunk * bins + lo, LANES), LANES)]
+        n = n + (re * re + im * im) * w
+    acc_ref[r : r + count, :] = n
 
 
 def norm_row(n):
@@ -80,7 +84,7 @@
     for chunk in range(chunks):
         fetch(chunk).start()
 
-    def gen(which, chunk):
+    def gen(which, chunk, beside=lambda i: None):
         a_ref, b_ref, y_ref = a_refs[which], b_refs[which], y_refs[which]
         shift = pl.multiple_of(chunk * kc, kc)
         w = w_ref[:, pl.ds(shift, kc)]
@@ -124,6 +128,7 @@
                     y_ref[at : at + total, kc + lo : kc + lo + LANES] = yi
                     y_ref[cols + at : cols + at + total, lo : lo + LANES] = yi
                     y_ref[cols + at : cols + at + total, kc + lo : kc + lo + LANES] = -yr
+            beside(lo // LANES)
 
     ids = base + lax.broadcasted_iota(jnp.int32, (PAIRS, kc), 1)
     odd = 2 * lax.broadcasted_iota(jnp.int32, (PAIRS, kc), 0) + 1
@@ -142,9 +147,8 @@
         fetch(2 * turn + 1).wait()
         for half in range(2):
             chunk = 2 * turn + half
-            gen(1 - half, jnp.minimum(chunk + 1, chunks - 1))
-            w = w_ref[:, pl.ds(pl.multiple_of(chunk * kc, kc), kc)]
-            norm_add(nacc_ref, w, lambda c, r, n, at: held_ref[chunk, c, r : r + n, at : at + LANES], kc)
+            beside = functools.partial(norm_add, nacc_ref, w_ref, held_ref, chunk, turns=kc // LANES)
+            gen(1 - half, jnp.minimum(chunk + 1, chunks - 1), beside)
             h = jnp.concatenate([held_ref[chunk, 0], held_ref[chunk, 1]], axis=1)
             acc_ref[...] += dot_t(h, y_refs[half][...])
         return carry
@@ -266,7 +270,7 @@
     for chunk in range(chunks):
         fetch(chunk).start()
 
-    def gen(which, chunk):
+    def gen(which, chunk, beside=lambda i: None):
         a_ref, b_ref, y_ref = a_refs[which], b_refs[which], y_refs[which]
         shift = pl.multiple_of(chunk * kc, kc)
         w = w_ref[:, pl.ds(shift, kc)]
@@ -298,6 +302,7 @@
                 y_ref[cols + at : cols + at + LAGS, lanes] = jnp.concatenate(
                     [jc + rs, jc - rs], axis=0
                 ).astype(BF16)
+            beside(lo // LANES)
 
     ids = base + lax.broadcasted_iota(jnp.int32, (PAIRS, kc), 1)
     odd = 2 * lax.broadcasted_iota(jnp.int32, (PAIRS, kc), 0) + 1
@@ -317,9 +322,8 @@
         fetch(2 * turn + 1).wait()
         for half in range(2):
             chunk = 2 * turn + half
-            gen(1 - half, jnp.minimum(chunk + 1, chunks - 1))
-            w = w_ref[:, pl.ds(pl.multiple_of(chunk * kc, kc), kc)]
-            norm_add(nacc_ref, w, lambda c, r, n, at: held_ref[chunk, c, r : r + n, at : at + LANES], kc)
+            beside = functools.partial(norm_add, nacc_ref, w_ref, held_ref, chunk, turns=kc // LANES)
+            gen(1 - half, jnp.minimum(chunk + 1, chunks - 1), beside)
             g = jnp.concatenate([held_ref[chunk, 0], held_ref[chunk, 1]], axis=0)
             acc_ref[...] += dot_t(y_refs[half][...], g)
         return carry
@@ -510,8 +514,9 @@
     )(fine_info, triggers.T, offsets.T, fine_spectra)
     order = sorted(range(banks), key=lambda k: min(k, banks - k))
     fine_blocks = {}
-    for k in order:
-        fine_blocks[k] = picked[k] if k == 0 else shift_permute(picked[k], "bank", banks, k)
+    for place, k in enumerate(order):
+        block = picked[k] if place < 2 else after(picked[k], *coarse_blocks)
+        fine_blocks[k] = block if k == 0 else shift_permute(block, "bank", banks, k)
 
     def exchange(send):
         return [shift_permute(send[k - 1 : k], "freq", freqs, k) for k in range(1, freqs)]

time: 92.5 us -> 92.1 us (level)
  starting transfers between devices: 27.9 us -> 15.3 us
  waiting for transfers between devices: 27.1 us -> 39.3 us
    ppermute x11, starting transfers between devices: 27.9 us -> 15.3 us  [shift_permute(): lax.ppermute(value, axis, [(i, (i + by) % count) for i in range(count)])]
    ppermute x11, waiting for transfers between devices: 27.1 us -> 39.3 us  [shift_permute(): lax.ppermute(value, axis, [(i, (i + by) % count) for i in range(count)])]
  transfers between devices with their start and end apart: 11 -> 11, of which waited for: 8 -> 9; matrix products, arithmetic and copies ran while one was open for 0% -> 0% of each run, Pallas kernels for 17% -> 17%
where the time goes in v2:
time: 92.1 us; the launch traced here: 91.9 us
  waiting for transfers between devices  39.3 us (43%)
  Pallas kernels  34.8 us (38%)
  starting transfers between devices  15.3 us (17%)
  local copies, waits for them, and re-layouts  1.68 us (2%)
    ppermute x11, waiting for transfers between devices, shift_permute(): lax.ppermute(value, axis, [(i, (i + by) % count) for i in range(count)])  39.3 us
    pallas_call x1, Pallas kernels, coarse_section(): pl.pallas_call(kernel, in_specs=[SMEM, VMEM, HBM] + [VMEM for _ in blocks...  17.8 us
    ppermute x11, starting transfers between devices, shift_permute(): lax.ppermute(value, axis, [(i, (i + by) % count) for i in range(count)])  15.3 us
    pallas_call x1, Pallas kernels, fine_section(): pl.pallas_call(kernel, in_specs=[SMEM, VMEM, VMEM, HBM] + [VMEM for _ in...  12.5 us
    pallas_call x1, Pallas kernels, body(): pl.pallas_call(functools.partial(pick_kernel, banks=banks, segs=segs, top...  2.3 us
  transfers between devices with their start and end apart: 11, of which 9 were waited for; matrix products, arithmetic and copies ran while one was open for 0% of the time, Pallas kernels for 17%

profile of v2, /device:TPU:0, one launch (start us, length us, event | category | flops | bytes accessed | tf_op | source)
XLA Modules:
  0.0 91.9 jit_solution(13525574818754282706)
XLA Ops:
  0.7 5.1 %collective-permute-start.2 = (bf16[4,2,8192]{2,1,0:T(2,128)(2,1)}, bf16[4,2,8192]{2,1,0:T(2,128)(2,1)S(1)}, u32[]{:S(2)}, u32[]{:S(2)}) collective-permute-start(bf16[4,2,8192]{2,1,0:T(2,128)(2,1)} %rest_0_.1), channel_id=1, source_target_pairs={{0,12},{4,0},{8,4},{12,8},{1,13},{5,1},{9,5},{13,9},{2,14},{6,2},{... | collective-permute-start | bytes 393224 | tf_op jit(solution)/shard_map/ppermute | solution.py:471
  5.8 1.0 %collective-permute-start = (bf16[4,2,8192]{2,1,0:T(2,128)(2,1)}, bf16[4,2,8192]{2,1,0:T(2,128)(2,1)S(1)}, u32[]{:S(2)}, u32[]{:S(2)}) collective-permute-start(bf16[4,2,8192]{2,1,0:T(2,128)(2,1)} %rest_0_.1), channel_id=1, source_target_pairs={{0,4},{4,8},{8,12},{12,0},{1,5},{5,9},{9,13},{13,1},{2,6},{6,10},{... | collective-permute-start | bytes 393224 | tf_op jit(solution)/shard_map/ppermute | solution.py:471
  6.9 3.1 %collective-permute-done.2.rest_3_ = bf16[4,2,8192]{2,1,0:T(2,128)(2,1)S(1)} collective-permute-done((bf16[4,2,8192]{2,1,0:T(2,128)(2,1)}, bf16[4,2,8192]{2,1,0:T(2,128)(2,1)S(1)}, u32[]{:S(2)}, u32[]{:S(2)}) %collective-permute-start.2) | collective-permute-done | bytes 131104 | tf_op jit(solution)/shard_map/ppermute | solution.py:471
  10.0 7.2 %collective-permute-done.1.rest_2_ = bf16[4,2,8192]{2,1,0:T(2,128)(2,1)S(1)} collective-permute-done((bf16[4,2,8192]{2,1,0:T(2,128)(2,1)}, bf16[4,2,8192]{2,1,0:T(2,128)(2,1)S(1)}, u32[]{:S(2)}, u32[]{:S(2)}) %collective-permute-start.1) | collective-permute-done | bytes 131104 | tf_op jit(solution)/shard_map/ppermute | solution.py:471
  17.2 0.9 copy-done.4
  18.1 0.8 copy-done.5
  18.9 17.8 %coarse.1 = (f32[264,512]{1,0:T(8,128)S(1)}, f32[1,264,512]{2,1,0:T(8,128)S(1)}) custom-call(s32[4]{0:T(128)S(1)} %pad_add_fusion.1.info_ref, f32[1,8192]{1,0:T(1,128)S(1)} %bitcast.13, bf16[2,512,8192]{2,1,0:T(8,128)(2,1)} %h_ref.1, bf16[4,2,8192]{2,1,0:T(2,128)(2,1)S(1)} %copy-done.4, bf16[4,2,8192]{2,1,0:T(2,128)(2,1)S(1)} %collective-permute-done.rest_1_, ...), custom_call_target="tpu_custom_call" | custom-call | flops 8589934592 | bytes 16777216 | tf_op jit(solution)/shard_map/coarse/pallas_call | solution.py:394
  36.7 1.6 %collective-permute-start.6 = (f32[1,264,512]{2,1,0:T(8,128)S(1)}, f32[1,264,512]{2,1,0:T(8,128)S(1)}, u32[]{:S(2)}, u32[]{:S(2)}) collective-permute-start(f32[1,264,512]{2,1,0:T(8,128)S(1)} %get-tuple-element.31), channel_id=1, source_target_pairs={{0,2},{2,0},{1,3},{3,1},{4,6},{6,4},{5,7},{7,5},{8,10},{10,8},{9,1... | collective-permute-start | bytes 1622024 | tf_op jit(solution)/shard_map/ppermute | solution.py:471
  38.3 2.3 %pick.1 = (bf16[2,2,32768]{2,1,0:T(2,128)(2,1)S(1)}, bf16[2,2,32768]{2,1,0:T(2,128)(2,1)S(1)}, bf16[2,2,32768]{2,1,0:T(2,128)(2,1)S(1)}, bf16[2,2,32768]{2,1,0:T(2,128)(2,1)S(1)}, s32[8,128]{1,0:T(8,128)S(1)}) custom-call(s32[4]{0:T(128)S(1)} %pad_add_fusion.info_ref, s32[2,16]{1,0:T(2,128)S(1)} %bitcast.10, s32[2,16]{1,0:T(2,128)S(1)} %bitcast.12, ...), custom_call_target="tpu_custom_call" | custom-call | tf_op jit(solution)/shard_map/pick/pallas_call | solution.py:506
  40.7 0.9 collective-permute-start.3
  41.5 3.0 %collective-permute-start.5 = (bf16[2,2,32768]{2,1,0:T(2,128)(2,1)S(1)}, bf16[2,2,32768]{2,1,0:T(2,128)(2,1)S(1)}, u32[]{:S(2)}, u32[]{:S(2)}) collective-permute-start(bf16[2,2,32768]{2,1,0:T(2,128)(2,1)S(1)} %get-tuple-element.28), channel_id=1, source_target_pairs={{0,12},{4,0},{8,4},{12,8},{1,13},{5,1},{9,5},{13,9},{2,14},{6,2},{... | collective-permute-start | bytes 786440 | tf_op jit(solution)/shard_map/ppermute | solution.py:471
  44.5 0.8 collective-permute-start.4
  45.3 6.4 %collective-permute-done.3.rest_1_ = bf16[2,2,32768]{2,1,0:T(2,128)(2,1)S(1)} collective-permute-done((bf16[2,2,32768]{2,1,0:T(2,128)(2,1)S(1)}, bf16[2,2,32768]{2,1,0:T(2,128)(2,1)S(1)}, u32[]{:S(2)}, u32[]{:S(2)}) %collective-permute-start.3) | collective-permute-done | bytes 262176 | tf_op jit(solution)/shard_map/ppermute | solution.py:471
  51.7 3.0 %collective-permute-done.5.rest_3_ = bf16[2,2,32768]{2,1,0:T(2,128)(2,1)S(1)} collective-permute-done((bf16[2,2,32768]{2,1,0:T(2,128)(2,1)S(1)}, bf16[2,2,32768]{2,1,0:T(2,128)(2,1)S(1)}, u32[]{:S(2)}, u32[]{:S(2)}) %collective-permute-start.5) | collective-permute-done | bytes 262176 | tf_op jit(solution)/shard_map/ppermute | solution.py:471
  54.7 12.0 %collective-permute-done.4.rest_2_ = bf16[2,2,32768]{2,1,0:T(2,128)(2,1)S(1)} collective-permute-done((bf16[2,2,32768]{2,1,0:T(2,128)(2,1)S(1)}, bf16[2,2,32768]{2,1,0:T(2,128)(2,1)S(1)}, u32[]{:S(2)}, u32[]{:S(2)}) %collective-permute-start.4) | collective-permute-done | bytes 262176 | tf_op jit(solution)/shard_map/ppermute | solution.py:471
  66.7 12.5 %fine.1 = (f32[136,128]{1,0:T(8,128)S(1)}, f32[1,136,128]{2,1,0:T(8,128)S(1)}) custom-call(s32[4]{0:T(128)S(1)} %pad_add_fusion.info_ref, f32[1,32768]{1,0:T(1,128)S(1)} %bitcast.9, s32[8,128]{1,0:T(8,128)S(1)} %get-tuple-element.22.mult_ref, bf16[2,1,64,32768]{3,2,1,0:T(8,128)(2,1)} %g_ref.1, bf16[2,2,32768]{2,1,0:T(2,128)(2,1)S(1)} %get-tuple-element.23.rest_0_, ...), custom_call_target="tpu_custom_call" | custom-call | flops 2147483648 | bytes 8388608 | tf_op jit(solution)/shard_map/fine/pallas_call | solution.py:435
  79.8 0.9 coarse_final.1
  80.7 2.9 %collective-permute-done.7.rest_0_ = f32[1,136,128]{2,1,0:T(8,128)S(1)} collective-permute-done((f32[1,136,128]{2,1,0:T(8,128)S(1)}, f32[1,136,128]{2,1,0:T(8,128)S(1)}, u32[]{:S(2)}, u32[]{:S(2)}) %collective-permute-start.7) | collective-permute-done | bytes 69664 | tf_op jit(solution)/shard_map/ppermute | solution.py:471
  83.6 1.7 %collective-permute-start.8 = (f32[2,128]{1,0:T(2,128)S(1)}, f32[2,128]{1,0:T(2,128)S(1)}, u32[]{:S(2)}, u32[]{:S(2)}) collective-permute-start(f32[2,128]{1,0:T(2,128)S(1)} %get-tuple-element.35), channel_id=1, source_target_pairs={{0,12},{4,0},{8,4},{12,8},{1,13},{5,1},{9,5},{13,9},{2,14},{6,2},{... | collective-permute-start | bytes 3080 | tf_op jit(solution)/shard_map/ppermute | solution.py:471
  85.3 0.6 collective-permute-start.10
  85.9 1.3 %collective-permute-done.8.rest_1_ = f32[2,128]{1,0:T(2,128)S(1)} collective-permute-done((f32[2,128]{1,0:T(2,128)S(1)}, f32[2,128]{1,0:T(2,128)S(1)}, u32[]{:S(2)}, u32[]{:S(2)}) %collective-permute-start.8) | collective-permute-done | bytes 1056 | tf_op jit(solution)/shard_map/ppermute | solution.py:471
  87.3 2.5 %collective-permute-done.9.rest_2_ = f32[2,128]{1,0:T(2,128)S(1)} collective-permute-done((f32[2,128]{1,0:T(2,128)S(1)}, f32[2,128]{1,0:T(2,128)S(1)}, u32[]{:S(2)}, u32[]{:S(2)}) %collective-permute-start.9) | collective-permute-done | bytes 1056 | tf_op jit(solution)/shard_map/ppermute | solution.py:471
  89.8 0.9 collective-permute-done.10.rest_3_
  90.7 1.2 %place.1 = f32[4,2,32]{2,1,0:T(2,128)} custom-call(s32[4]{0:T(128)S(1)} %pad_add_fusion.info_ref, s32[2,16]{1,0:T(2,128)S(1)} %bitcast.11, f32[2,128]{1,0:T(2,128)S(1)} %get-tuple-element.34.rest_0_, f32[2,128]{1,0:T(2,128)S(1)} %collective-permute-done.8.rest_1_, f32[2,128]{1,0:T(2,128)S(1)} %collective-permute-done.9.rest_2_, ...), custom_call_target="tpu_custom_call" | custom-call | tf_op jit(solution)/shard_map/place/pallas_call | solution.py:554
  (18 shorter events, 0.9 us)
Async XLA Ops:
  0.6 37.7 %copy-start.3 = (s32[16,2]{0,1:T(2,128)S(1)}, s32[16,2]{0,1:T(2,128)}, u32[]{:S(2)}) copy-start(s32[16,2]{0,1:T(2,128)} %param.15) | copy-start | bytes 388
  0.6 37.7 %copy-start.2 = (s32[16,2]{0,1:T(2,128)S(1)}, s32[16,2]{0,1:T(2,128)}, u32[]{:S(2)}) copy-start(s32[16,2]{0,1:T(2,128)} %param.14) | copy-start | bytes 388
  0.7 37.7 %copy-start = (bf16[4,2,32768]{2,1,0:T(2,128)(2,1)S(1)}, bf16[4,2,32768]{2,1,0:T(2,128)(2,1)}, u32[]{:S(2)}) copy-start(bf16[4,2,32768]{2,1,0:T(2,128)(2,1)} %spec_ref.1) | copy-start | bytes 1572868
  0.7 66.0 %copy-start.1 = (f32[32768]{0:T(1024)S(1)}, f32[32768]{0:T(1024)}, u32[]{:S(2)}) copy-start(f32[32768]{0:T(1024)} %param.13) | copy-start | bytes 393220
  0.7 9.3 %collective-permute-start.2 = (bf16[4,2,8192]{2,1,0:T(2,128)(2,1)}, bf16[4,2,8192]{2,1,0:T(2,128)(2,1)S(1)}, u32[]{:S(2)}, u32[]{:S(2)}) collective-permute-start(bf16[4,2,8192]{2,1,0:T(2,128)(2,1)} %rest_0_.1), channel_id=1, source_target_pairs={{0,12},{4,0},{8,4},{12,8},{1,13},{5,1},{9,5},{13,9},{2,14},{6,2},{... | collective-permute-start | bytes 393224 | tf_op jit(solution)/shard_map/ppermute | solution.py:471
  5.8 11.4 %collective-permute-start.1 = (bf16[4,2,8192]{2,1,0:T(2,128)(2,1)}, bf16[4,2,8192]{2,1,0:T(2,128)(2,1)S(1)}, u32[]{:S(2)}, u32[]{:S(2)}) collective-permute-start(bf16[4,2,8192]{2,1,0:T(2,128)(2,1)} %rest_0_.1), channel_id=1, source_target_pairs={{0,8},{4,12},{8,0},{12,4},{1,9},{5,13},{9,1},{13,5},{2,10},{6,14},... | collective-permute-start | bytes 393224 | tf_op jit(solution)/shard_map/ppermute | solution.py:471
  5.8 11.4 %collective-permute-start = (bf16[4,2,8192]{2,1,0:T(2,128)(2,1)}, bf16[4,2,8192]{2,1,0:T(2,128)(2,1)S(1)}, u32[]{:S(2)}, u32[]{:S(2)}) collective-permute-start(bf16[4,2,8192]{2,1,0:T(2,128)(2,1)} %rest_0_.1), channel_id=1, source_target_pairs={{0,4},{4,8},{8,12},{12,0},{1,5},{5,9},{9,13},{13,1},{2,6},{6,10},{... | collective-permute-start | bytes 393224 | tf_op jit(solution)/shard_map/ppermute | solution.py:471
  17.2 0.9 copy-start.4
  18.1 0.8 copy-start.5
  36.7 43.1 %collective-permute-start.6 = (f32[1,264,512]{2,1,0:T(8,128)S(1)}, f32[1,264,512]{2,1,0:T(8,128)S(1)}, u32[]{:S(2)}, u32[]{:S(2)}) collective-permute-start(f32[1,264,512]{2,1,0:T(8,128)S(1)} %get-tuple-element.31), channel_id=1, source_target_pairs={{0,2},{2,0},{1,3},{3,1},{4,6},{6,4},{5,7},{7,5},{8,10},{10,8},{9,1... | collective-permute-start | bytes 1622024 | tf_op jit(solution)/shard_map/ppermute | solution.py:471
  40.7 11.1 %collective-permute-start.3 = (bf16[2,2,32768]{2,1,0:T(2,128)(2,1)S(1)}, bf16[2,2,32768]{2,1,0:T(2,128)(2,1)S(1)}, u32[]{:S(2)}, u32[]{:S(2)}) collective-permute-start(bf16[2,2,32768]{2,1,0:T(2,128)(2,1)S(1)} %get-tuple-element.24), channel_id=1, source_target_pairs={{0,4},{4,8},{8,12},{12,0},{1,5},{5,9},{9,13},{13,1},{2,6},{6,10},{... | collective-permute-start | bytes 786440 | tf_op jit(solution)/shard_map/ppermute | solution.py:471
  41.5 13.2 %collective-permute-start.5 = (bf16[2,2,32768]{2,1,0:T(2,128)(2,1)S(1)}, bf16[2,2,32768]{2,1,0:T(2,128)(2,1)S(1)}, u32[]{:S(2)}, u32[]{:S(2)}) collective-permute-start(bf16[2,2,32768]{2,1,0:T(2,128)(2,1)S(1)} %get-tuple-element.28), channel_id=1, source_target_pairs={{0,12},{4,0},{8,4},{12,8},{1,13},{5,1},{9,5},{13,9},{2,14},{6,2},{... | collective-permute-start | bytes 786440 | tf_op jit(solution)/shard_map/ppermute | solution.py:471
  44.5 22.2 %collective-permute-start.4 = (bf16[2,2,32768]{2,1,0:T(2,128)(2,1)S(1)}, bf16[2,2,32768]{2,1,0:T(2,128)(2,1)S(1)}, u32[]{:S(2)}, u32[]{:S(2)}) collective-permute-start(bf16[2,2,32768]{2,1,0:T(2,128)(2,1)S(1)} %get-tuple-element.26), channel_id=1, source_target_pairs={{0,8},{4,12},{8,0},{12,4},{1,9},{5,13},{9,1},{13,5},{2,10},{6,14},... | collective-permute-start | bytes 786440 | tf_op jit(solution)/shard_map/ppermute | solution.py:471
  79.2 4.4 %collective-permute-start.7 = (f32[1,136,128]{2,1,0:T(8,128)S(1)}, f32[1,136,128]{2,1,0:T(8,128)S(1)}, u32[]{:S(2)}, u32[]{:S(2)}) collective-permute-start(f32[1,136,128]{2,1,0:T(8,128)S(1)} %get-tuple-element.33), channel_id=1, source_target_pairs={{0,2},{2,0},{1,3},{3,1},{4,6},{6,4},{5,7},{7,5},{8,10},{10,8},{9,1... | collective-permute-start | bytes 208904 | tf_op jit(solution)/shard_map/ppermute | solution.py:471
  83.6 3.6 %collective-permute-start.8 = (f32[2,128]{1,0:T(2,128)S(1)}, f32[2,128]{1,0:T(2,128)S(1)}, u32[]{:S(2)}, u32[]{:S(2)}) collective-permute-start(f32[2,128]{1,0:T(2,128)S(1)} %get-tuple-element.35), channel_id=1, source_target_pairs={{0,12},{4,0},{8,4},{12,8},{1,13},{5,1},{9,5},{13,9},{2,14},{6,2},{... | collective-permute-start | bytes 3080 | tf_op jit(solution)/shard_map/ppermute | solution.py:471
  85.3 4.5 %collective-permute-start.9 = (f32[2,128]{1,0:T(2,128)S(1)}, f32[2,128]{1,0:T(2,128)S(1)}, u32[]{:S(2)}, u32[]{:S(2)}) collective-permute-start(f32[2,128]{1,0:T(2,128)S(1)} %get-tuple-element.36), channel_id=1, source_target_pairs={{0,8},{4,12},{8,0},{12,4},{1,9},{5,13},{9,1},{13,5},{2,10},{6,14},... | collective-permute-start | bytes 3080 | tf_op jit(solution)/shard_map/ppermute | solution.py:471
  85.3 5.4 %collective-permute-start.10 = (f32[2,128]{1,0:T(2,128)S(1)}, f32[2,128]{1,0:T(2,128)S(1)}, u32[]{:S(2)}, u32[]{:S(2)}) collective-permute-start(f32[2,128]{1,0:T(2,128)S(1)} %get-tuple-element.37), channel_id=1, source_target_pairs={{0,4},{4,8},{8,12},{12,0},{1,5},{5,9},{9,13},{13,1},{2,6},{6,10},{... | collective-permute-start | bytes 3080 | tf_op jit(solution)/shard_map/ppermute | solution.py:471

commit v3 on v2

--- a/solution.py
+++ b/solution.py
@@ -70,7 +70,7 @@
     spec_refs = rest[:blocks]
     keep_ref, send_ref = rest[blocks : blocks + 2]
     a_refs, b_refs, y_refs = (rest[blocks + i : blocks + i + 2] for i in (2, 4, 6))
-    acc_ref, nacc_ref, tab_ref, ctr_ref, held_ref, sems = rest[blocks + 8 :]
+    acc_ref, tab_ref, ctr_ref, held_ref, sems = rest[blocks + 8 :]
     base = info_ref[0]
     bank = info_ref[1]
     freq = info_ref[2]
@@ -84,7 +84,7 @@
     for chunk in range(chunks):
         fetch(chunk).start()
 
-    def gen(which, chunk, beside=lambda i: None):
+    def gen(which, chunk):
         a_ref, b_ref, y_ref = a_refs[which], b_refs[which], y_refs[which]
         shift = pl.multiple_of(chunk * kc, kc)
         w = w_ref[:, pl.ds(shift, kc)]
@@ -128,7 +128,6 @@
                     y_ref[at : at + total, kc + lo : kc + lo + LANES] = yi
                     y_ref[cols + at : cols + at + total, lo : lo + LANES] = yi
                     y_ref[cols + at : cols + at + total, kc + lo : kc + lo + LANES] = -yr
-            beside(lo // LANES)
 
     ids = base + lax.broadcasted_iota(jnp.int32, (PAIRS, kc), 1)
     odd = 2 * lax.broadcasted_iota(jnp.int32, (PAIRS, kc), 0) + 1
@@ -139,7 +138,6 @@
     ctr_ref[0] = c
     ctr_ref[1] = s
     acc_ref[...] = jnp.zeros_like(acc_ref)
-    nacc_ref[...] = jnp.zeros_like(nacc_ref)
     gen(0, jnp.int32(0))
 
     def pair(turn, carry):
@@ -147,37 +145,74 @@
         fetch(2 * turn + 1).wait()
         for half in range(2):
             chunk = 2 * turn + half
-            beside = functools.partial(norm_add, nacc_ref, w_ref, held_ref, chunk, turns=kc // LANES)
-            gen(1 - half, jnp.minimum(chunk + 1, chunks - 1), beside)
+            gen(1 - half, jnp.minimum(chunk + 1, chunks - 1))
             h = jnp.concatenate([held_ref[chunk, 0], held_ref[chunk, 1]], axis=1)
             acc_ref[...] += dot_t(h, y_refs[half][...])
         return carry
 
     lax.fori_loop(0, chunks // 2, pair, 0)
     part = acc_ref.shape[0] // freqs
+    keep_ref[...] = acc_ref[pl.ds(pl.multiple_of(freq * part, part), part), :]
+    for k in range(1, freqs):
+        dest = pl.multiple_of(lax.rem(freq + k, freqs) * part, part)
+        send_ref[k - 1] = acc_ref[pl.ds(dest, part), :]
+
+
+def norm_kernel(
+    info_ref, cw_ref, fw_ref, h_ref, g_ref, keep_ref, send_ref, c_ref, f_ref, h_held, g_held, h_sems, g_sems, *, freqs
+):
+    chunks, _, rows, kc = h_held.shape
+    tsub, kf = g_held.shape[2:]
+
+    def fetch(i):
+        at = pl.ds(pl.multiple_of(i * kc, kc), kc)
+        yield pltpu.make_async_copy(h_ref.at[:, :, at], h_held.at[i], h_sems.at[i])
+        at = pl.ds(pl.multiple_of(i * kf, kf), kf)
+        yield pltpu.make_async_copy(g_ref.at[:, 0, :, at], g_held.at[i], g_sems.at[i])
+
+    for i in range(chunks):
+        for copy in fetch(i):
+            copy.start()
+    c_ref[...] = jnp.zeros_like(c_ref)
+    f_ref[...] = jnp.zeros_like(f_ref)
+
+    def turn(i, carry):
+        for copy in fetch(i):
+            copy.wait()
+        for t in range(8):
+            norm_add(c_ref, cw_ref, h_held, i, t, 8)
+        for t in range(4):
+            norm_add(f_ref, fw_ref, g_held, i, t, 4)
+        return carry
+
+    lax.fori_loop(0, chunks, turn, 0)
+    part = rows // freqs
+    fine_part = tsub // freqs
     size = min(part, LANES)
 
     def lay(ref, dest):
-        first = pl.multiple_of(dest * part, part)
-        ref[:part, :] = acc_ref[pl.ds(first, part), :]
+        ref[...] = jnp.zeros_like(ref)
         for r in range(0, part, size):
-            row = norm_row(nacc_ref[pl.ds(first + r, size), :])
-            ref[part : part + 8, r : r + LANES] = jnp.broadcast_to(row, (8, LANES))
-
-    lay(keep_ref, freq)
+            row = norm_row(c_ref[pl.ds(pl.multiple_of(dest * part + r, size), size), :])
+            ref[r // size : r // size + 1, :] = row
+        row = norm_row(f_ref[pl.ds(pl.multiple_of(dest * fine_part, fine_part), fine_part), :])
+        ref[part // size : part // size + 1, :] = row
+
+    lay(keep_ref, info_ref[2])
     for k in range(1, freqs):
-        lay(send_ref.at[k - 1], lax.rem(freq + k, freqs))
-
-
-def coarse_final_kernel(keep_ref, *rest, freqs, total):
-    recv_refs = rest[: freqs - 1]
-    out_ref = rest[freqs - 1]
-    part = keep_ref.shape[0] - 8
+        lay(send_ref.at[k - 1], lax.rem(info_ref[2] + k, freqs))
+
+
+def coarse_final_kernel(keep_ref, norm_ref, *rest, freqs, total):
+    recv_refs = rest[: 2 * (freqs - 1)]
+    out_ref = rest[2 * (freqs - 1)]
+    part = keep_ref.shape[0]
     cols = total * LAGS
     corr = keep_ref[...]
-    for ref in recv_refs:
-        corr = corr + ref[0]
-    norms = corr[part : part + 1]
+    norms = norm_ref[...]
+    for k in range(freqs - 1):
+        corr = corr + recv_refs[2 * k][0]
+        norms = norms + recv_refs[2 * k + 1][0]
     cr = corr[:part, :cols]
     ci = corr[:part, cols:]
     e = cr * cr + ci * ci
@@ -193,7 +228,7 @@
         rows = e[r : r + size]
         if size < LANES:
             rows = jnp.concatenate([rows, jnp.zeros((LANES - size, LANES), F32)], axis=0)
-        out = rows.T[:total] / norms[:, r : r + LANES]
+        out = rows.T[:total] / norms[r // size : r // size + 1]
         out_ref[:, r : r + size] = out[:, :size]
 
 
@@ -256,7 +291,7 @@
     slot_refs = rest[:blocks]
     keep_ref, send_ref = rest[blocks : blocks + 2]
     a_refs, b_refs, y_refs = (rest[blocks + i : blocks + i + 2] for i in (2, 4, 6))
-    acc_ref, nacc_ref, tab_ref, ctr_ref, held_ref, sems = rest[blocks + 8 :]
+    acc_ref, tab_ref, ctr_ref, held_ref, sems = rest[blocks + 8 :]
     base = info_ref[0]
     freq = info_ref[2]
     n = blocks * CAP
@@ -270,7 +305,7 @@
     for chunk in range(chunks):
         fetch(chunk).start()
 
-    def gen(which, chunk, beside=lambda i: None):
+    def gen(which, chunk):
         a_ref, b_ref, y_ref = a_refs[which], b_refs[which], y_refs[which]
         shift = pl.multiple_of(chunk * kc, kc)
         w = w_ref[:, pl.ds(shift, kc)]
@@ -302,7 +337,6 @@
                 y_ref[cols + at : cols + at + LAGS, lanes] = jnp.concatenate(
                     [jc + rs, jc - rs], axis=0
                 ).astype(BF16)
-            beside(lo // LANES)
 
     ids = base + lax.broadcasted_iota(jnp.int32, (PAIRS, kc), 1)
     odd = 2 * lax.broadcasted_iota(jnp.int32, (PAIRS, kc), 0) + 1
@@ -314,7 +348,6 @@
     ctr_ref[0] = c
     ctr_ref[1] = s
     acc_ref[...] = jnp.zeros_like(acc_ref)
-    nacc_ref[...] = jnp.zeros_like(nacc_ref)
     gen(0, jnp.int32(0))
 
     def pair(turn, carry):
@@ -322,8 +355,7 @@
         fetch(2 * turn + 1).wait()
         for half in range(2):
             chunk = 2 * turn + half
-            beside = functools.partial(norm_add, nacc_ref, w_ref, held_ref, chunk, turns=kc // LANES)
-            gen(1 - half, jnp.minimum(chunk + 1, chunks - 1), beside)
+            gen(1 - half, jnp.minimum(chunk + 1, chunks - 1))
             g = jnp.concatenate([held_ref[chunk, 0], held_ref[chunk, 1]], axis=0)
             acc_ref[...] += dot_t(y_refs[half][...], g)
         return carry
@@ -335,7 +367,6 @@
     corr_real = acc[:cols] + swap[cols:]
     corr_imag = acc[cols:] - swap[:cols]
     lane = lax.broadcasted_iota(jnp.int32, (1, LANES), 1)
-    norms = jnp.broadcast_to(norm_row(nacc_ref[...]), (8, LANES))
 
     def pack(dest):
         real, imag = corr_real, pltpu.roll(corr_imag, part, 1)
@@ -344,25 +375,21 @@
             real = jnp.where(here, pltpu.roll(corr_real, LANES - d * part, 1), real)
             moved = corr_imag if d == 1 else pltpu.roll(corr_imag, LANES - (d - 1) * part, 1)
             imag = jnp.where(here, moved, imag)
-        row = norms
-        for d in range(1, freqs):
-            row = jnp.where(dest == d, pltpu.roll(norms, LANES - d * part, 1), row)
-        return jnp.concatenate(
-            [jnp.where(lane < part, real, jnp.where(lane < 2 * part, imag, 0.0)), row], axis=0
-        )
+        return jnp.where(lane < part, real, jnp.where(lane < 2 * part, imag, 0.0))
 
     keep_ref[...] = pack(freq)
     for k in range(1, freqs):
         send_ref[k - 1] = pack(lax.rem(freq + k, freqs))
 
 
-def fine_final_kernel(keep_ref, *rest, freqs, n, part):
-    recv_refs = rest[: freqs - 1]
-    out_refs = rest[freqs - 1 :]
+def fine_final_kernel(keep_ref, norm_ref, *rest, freqs, n, part, line):
+    recv_refs = rest[: 2 * (freqs - 1)]
+    out_refs = rest[2 * (freqs - 1) :]
     x = keep_ref[...]
-    for ref in recv_refs:
-        x = x + ref[0]
-    norm = x[n * LAGS : n * LAGS + 1]
+    norm = norm_ref[line : line + 1, :]
+    for k in range(freqs - 1):
+        x = x + recv_refs[2 * k][0]
+        norm = norm + recv_refs[2 * k + 1][0, line : line + 1, :]
     e = x[: n * LAGS]
     e = e * e
     e = e + pltpu.roll(e, LANES - part, 1)
@@ -400,15 +427,14 @@
         ]
         + [VMEM for _ in blocks],
         out_shape=[
-            jax.ShapeDtypeStruct((part + 8, 2 * cols), F32),
-            jax.ShapeDtypeStruct((freqs - 1, part + 8, 2 * cols), F32),
+            jax.ShapeDtypeStruct((part, 2 * cols), F32),
+            jax.ShapeDtypeStruct((freqs - 1, part, 2 * cols), F32),
         ],
         scratch_shapes=[
             *[pltpu.VMEM((banks, 2 * segs, kc), F32) for _ in range(2)],
             *[pltpu.VMEM((4, total, kc), F32) for _ in range(2)],
             *[pltpu.VMEM((2 * cols, 2 * kc), BF16) for _ in range(2)],
             pltpu.VMEM((rows, 2 * cols), F32),
-            pltpu.VMEM((rows, LANES), F32),
             pltpu.VMEM((2, PAIRS, kc), F32),
             pltpu.VMEM((2, PAIRS, kc), F32),
             pltpu.VMEM((chunks, 2, rows, kc), BF16),
@@ -442,14 +468,13 @@
         ]
         + [VMEM for _ in blocks],
         out_shape=[
-            jax.ShapeDtypeStruct((cols + 8, LANES), F32),
-            jax.ShapeDtypeStruct((freqs - 1, cols + 8, LANES), F32),
+            jax.ShapeDtypeStruct((cols, LANES), F32),
+            jax.ShapeDtypeStruct((freqs - 1, cols, LANES), F32),
         ],
         scratch_shapes=[
             *[pltpu.VMEM((2, n, kc), F32) for _ in range(4)],
             *[pltpu.VMEM((2 * cols, kc), BF16) for _ in range(2)],
             pltpu.VMEM((2 * cols, LANES), F32),
-            pltpu.VMEM((tsub, LANES), F32),
             pltpu.VMEM((2, PAIRS, kc), F32),
             pltpu.VMEM((2, n, kc), F32),
             pltpu.VMEM((chunks, 2, tsub, kc), BF16),
@@ -469,6 +494,34 @@
 
 def shift_permute(value, axis, count, by):
     return lax.ppermute(value, axis, [(i, (i + by) % count) for i in range(count)])
+
+
+def norm_section(info, coarse_weight, fine_weight, coarse_templates, fine_templates, freqs):
+    rows, bins = coarse_templates.shape[1:]
+    tsub, fine_bins = fine_templates.shape[2:]
+    chunks = 8
+    lines = -(-(max(rows // freqs // LANES, 1) + 1) // 8) * 8
+    return pl.pallas_call(
+        functools.partial(norm_kernel, freqs=freqs),
+        in_specs=[SMEM, VMEM, VMEM, HBM, HBM],
+        out_shape=[
+            jax.ShapeDtypeStruct((lines, LANES), F32),
+            jax.ShapeDtypeStruct((freqs - 1, lines, LANES), F32),
+        ],
+        scratch_shapes=[
+            pltpu.VMEM((rows, LANES), F32),
+            pltpu.VMEM((tsub, LANES), F32),
+            pltpu.VMEM((chunks, 2, rows, bins // chunks), BF16),
+            pltpu.VMEM((chunks, 2, tsub, fine_bins // chunks), BF16),
+            pltpu.SemaphoreType.DMA((chunks,)),
+            pltpu.SemaphoreType.DMA((chunks,)),
+        ],
+        compiler_params=params(),
+        cost_estimate=pl.CostEstimate(
+            flops=10**9, bytes_accessed=4 * (rows * bins + tsub * fine_bins), transcendentals=0
+        ),
+        name="norms",
+    )(info, coarse_weight, fine_weight, coarse_templates, fine_templates)
 
 
 def body(
@@ -518,11 +571,17 @@
         block = picked[k] if place < 2 else after(picked[k], *coarse_blocks)
         fine_blocks[k] = block if k == 0 else shift_permute(block, "bank", banks, k)
 
+    line = max(coarse_templates.shape[1] // freqs // LANES, 1)
+
     def exchange(send):
         return [shift_permute(send[k - 1 : k], "freq", freqs, k) for k in range(1, freqs)]
 
+    norms, send_norms = norm_section(
+        after(coarse_info, mult), coarse_weight, fine_weight, coarse_templates, fine_templates, freqs
+    )
+    recv_norms = exchange(send_norms)
     keep, send = coarse_section(
-        coarse_info, coarse_weight, coarse_templates, coarse_blocks, banks, freqs, coarse_period
+        after(coarse_info, norms), coarse_weight, coarse_templates, coarse_blocks, banks, freqs, coarse_period
     )
     coarse_keep, coarse_received = keep, exchange(send)
     keep, send = fine_section(
@@ -537,16 +596,16 @@
     received = exchange(send)
     coarse_snr = pl.pallas_call(
         functools.partial(coarse_final_kernel, freqs=freqs, total=banks * segs),
-        out_shape=jax.ShapeDtypeStruct((banks * segs, coarse_keep.shape[0] - 8), F32),
+        out_shape=jax.ShapeDtypeStruct((banks * segs, coarse_keep.shape[0]), F32),
         compiler_params=params(16),
         name="coarse_final",
-    )(after(coarse_keep, keep), *coarse_received)
+    )(after(coarse_keep, keep), norms, *[x for pair in zip(coarse_received, recv_norms) for x in pair])
     results = pl.pallas_call(
-        functools.partial(fine_final_kernel, freqs=freqs, n=CAP * banks, part=part),
+        functools.partial(fine_final_kernel, freqs=freqs, n=CAP * banks, part=part, line=line),
         out_shape=[jax.ShapeDtypeStruct((CAP, LANES), F32) for _ in range(banks)],
         compiler_params=params(8),
         name="fine_final",
-    )(after(keep, coarse_snr), *received)
+    )(after(keep, coarse_snr), norms, *[x for pair in zip(received, recv_norms) for x in pair])
     back = [
         results[k] if k == 0 else shift_permute(results[k], "bank", banks, banks - k)
         for k in range(banks)

time: 92.1 us -> 70.6 us (0.77)
  waiting for transfers between devices: 39.3 us -> 8.56 us
  Pallas kernels: 34.8 us -> 38.9 us
  starting transfers between devices: 15.3 us -> 18 us
  local copies, waits for them, and re-layouts: 1.68 us -> 4.08 us
    ppermute x11 -> x12, waiting for transfers between devices: 39.3 us -> 8.56 us  [shift_permute(): lax.ppermute(value, axis, [(i, (i + by) % count) for i in range(count)])]
    pallas_call x0 -> x1, Pallas kernels: none -> 9.8 us  [norm_section(): pl.pallas_call(functools.partial(norm_kernel, freqs=freqs), in_specs=[SME...]
    pallas_call x1, Pallas kernels: 17.8 us -> 14.1 us  [coarse_section(): pl.pallas_call(kernel, in_specs=[SMEM, VMEM, HBM] + [VMEM for _ in blocks...]
    ppermute x11 -> x12, starting transfers between devices: 15.3 us -> 18 us  [shift_permute(): lax.ppermute(value, axis, [(i, (i + by) % count) for i in range(count)])]
    unnamed x12 -> x16, local copies, waits for them, and re-layouts: 1.68 us -> 4.08 us
    pallas_call x1, Pallas kernels: 12.5 us -> 10.5 us  [fine_section(): pl.pallas_call(kernel, in_specs=[SMEM, VMEM, VMEM, HBM] + [VMEM for _ in...]
  transfers between devices with their start and end apart: 11 -> 12, of which waited for: 9 -> 5; matrix products, arithmetic and copies ran while one was open for 0% -> 0% of each run, Pallas kernels for 17% -> 53%
where the time goes in v3:
time: 70.6 us; the launch traced here: 70.3 us
  Pallas kernels  38.9 us (55%)
  starting transfers between devices  18 us (25%)
  waiting for transfers between devices  8.56 us (12%)
  local copies, waits for them, and re-layouts  4.08 us (6%)
  between operations  0.73 us (1%)
    ppermute x12, starting transfers between devices, shift_permute(): lax.ppermute(value, axis, [(i, (i + by) % count) for i in range(count)])  18 us
    pallas_call x1, Pallas kernels, coarse_section(): pl.pallas_call(kernel, in_specs=[SMEM, VMEM, HBM] + [VMEM for _ in blocks...  14.1 us
    pallas_call x1, Pallas kernels, fine_section(): pl.pallas_call(kernel, in_specs=[SMEM, VMEM, VMEM, HBM] + [VMEM for _ in...  10.5 us
    pallas_call x1, Pallas kernels, norm_section(): pl.pallas_call(functools.partial(norm_kernel, freqs=freqs), in_specs=[SME...  9.8 us
    ppermute x12, waiting for transfers between devices, shift_permute(): lax.ppermute(value, axis, [(i, (i + by) % count) for i in range(count)])  8.56 us
    unnamed x16, local copies, waits for them, and re-layouts  4.08 us
    pallas_call x1, Pallas kernels, body(): pl.pallas_call(functools.partial(pick_kernel, banks=banks, segs=segs, top...  2.29 us
  transfers between devices with their start and end apart: 12, of which 5 were waited for; matrix products, arithmetic and copies ran while one was open for 0% of the time, Pallas kernels for 53%

profile of v3, /device:TPU:0, one launch (start us, length us, event | category | flops | bytes accessed | tf_op | source)
XLA Modules:
  0.0 70.3 jit_solution(10817411360490569143)
XLA Ops:
  0.6 5.1 %collective-permute-start.2 = (bf16[4,2,8192]{2,1,0:T(2,128)(2,1)}, bf16[4,2,8192]{2,1,0:T(2,128)(2,1)S(1)}, u32[]{:S(2)}, u32[]{:S(2)}) collective-permute-start(bf16[4,2,8192]{2,1,0:T(2,128)(2,1)} %rest_0_.1), channel_id=1, source_target_pairs={{0,12},{4,0},{8,4},{12,8},{1,13},{5,1},{9,5},{13,9},{2,14},{6,2},{... | collective-permute-start | bytes 393224 | tf_op jit(solution)/shard_map/ppermute | solution.py:496
  5.8 1.0 %collective-permute-start = (bf16[4,2,8192]{2,1,0:T(2,128)(2,1)}, bf16[4,2,8192]{2,1,0:T(2,128)(2,1)S(1)}, u32[]{:S(2)}, u32[]{:S(2)}) collective-permute-start(bf16[4,2,8192]{2,1,0:T(2,128)(2,1)} %rest_0_.1), channel_id=1, source_target_pairs={{0,4},{4,8},{8,12},{12,0},{1,5},{5,9},{9,13},{13,1},{2,6},{6,10},{... | collective-permute-start | bytes 393224 | tf_op jit(solution)/shard_map/ppermute | solution.py:496
  6.9 1.0 %copy-done.2 = bf16[4,2,32768]{2,1,0:T(2,128)(2,1)S(1)} copy-done((bf16[4,2,32768]{2,1,0:T(2,128)(2,1)S(1)}, bf16[4,2,32768]{2,1,0:T(2,128)(2,1)}, u32[]{:S(2)}) %copy-start.2) | copy-done | bytes 524312
  7.9 0.7 copy-done.4
  8.6 0.7 copy-done.6
  9.3 2.3 %pick.1 = (bf16[2,2,32768]{2,1,0:T(2,128)(2,1)S(1)}, bf16[2,2,32768]{2,1,0:T(2,128)(2,1)S(1)}, bf16[2,2,32768]{2,1,0:T(2,128)(2,1)S(1)}, bf16[2,2,32768]{2,1,0:T(2,128)(2,1)S(1)}, s32[8,128]{1,0:T(8,128)S(1)}) custom-call(s32[4]{0:T(128)S(1)} %pad_add_fusion.info_ref, s32[2,16]{1,0:T(2,128)S(1)} %bitcast.13, s32[2,16]{1,0:T(2,128)S(1)} %bitcast.15, ...), custom_call_target="tpu_custom_call" | custom-call | tf_op jit(solution)/shard_map/pick/pallas_call | solution.py:559
  11.6 2.5 %collective-permute-start.3 = (bf16[2,2,32768]{2,1,0:T(2,128)(2,1)S(1)}, bf16[2,2,32768]{2,1,0:T(2,128)(2,1)S(1)}, u32[]{:S(2)}, u32[]{:S(2)}) collective-permute-start(bf16[2,2,32768]{2,1,0:T(2,128)(2,1)S(1)} %get-tuple-element.31), channel_id=1, source_target_pairs={{0,4},{4,8},{8,12},{12,0},{1,5},{5,9},{9,13},{13,1},{2,6},{6,10},{... | collective-permute-start | bytes 786440 | tf_op jit(solution)/shard_map/ppermute | solution.py:496
  14.2 0.9 %copy-done = f32[32768]{0:T(1024)S(1)} copy-done((f32[32768]{0:T(1024)S(1)}, f32[32768]{0:T(1024)}, u32[]{:S(2)}) %copy-start) | copy-done | bytes 131096
  15.1 0.8 %copy-done.3 = f32[8192]{0:T(1024)S(1)} copy-done((f32[8192]{0:T(1024)S(1)}, f32[8192]{0:T(1024)}, u32[]{:S(2)}) %copy-start.3) | copy-done | bytes 32792
  15.8 9.8 %norms.1 = (f32[8,128]{1,0:T(8,128)S(1)}, f32[1,8,128]{2,1,0:T(8,128)S(1)}) custom-call(s32[4]{0:T(128)S(1)} %pad_add_fusion.1.info_ref, f32[1,8192]{1,0:T(1,128)S(1)} %bitcast.11, f32[1,32768]{1,0:T(1,128)S(1)} %bitcast.9, bf16[2,512,8192]{2,1,0:T(8,128)(2,1)} %h_ref.3, bf16[2,1,64,32768]{3,2,1,0:T(8,128)(2,1)} %g_ref.3), custom_call_target="tpu_custom_call" | custom-call | flops 1000000000 | bytes 25165824 | tf_op jit(solution)/shard_map/norms/pallas_call | solution.py:504
  25.7 1.4 %collective-permute-start.5 = (bf16[2,2,32768]{2,1,0:T(2,128)(2,1)S(1)}, bf16[2,2,32768]{2,1,0:T(2,128)(2,1)S(1)}, u32[]{:S(2)}, u32[]{:S(2)}) collective-permute-start(bf16[2,2,32768]{2,1,0:T(2,128)(2,1)S(1)} %get-tuple-element.35), channel_id=1, source_target_pairs={{0,12},{4,0},{8,4},{12,8},{1,13},{5,1},{9,5},{13,9},{2,14},{6,2},{... | collective-permute-start | bytes 786440 | tf_op jit(solution)/shard_map/ppermute | solution.py:496
  27.2 14.1 %coarse.1 = (f32[256,512]{1,0:T(8,128)S(1)}, f32[1,256,512]{2,1,0:T(8,128)S(1)}) custom-call(s32[4]{0:T(128)S(1)} %pad_add_fusion.1.info_ref, f32[1,8192]{1,0:T(1,128)S(1)} %bitcast.12, bf16[2,512,8192]{2,1,0:T(8,128)(2,1)} %h_ref.3, bf16[4,2,8192]{2,1,0:T(2,128)(2,1)S(1)} %copy-done.7, bf16[4,2,8192]{2,1,0:T(2,128)(2,1)S(1)} %collective-permute-done.rest_1_, ...), custom_call_target="tpu_custom_call" | custom-call | flops 8589934592 | bytes 16777216 | tf_op jit(solution)/shard_map/coarse/pallas_call | solution.py:421
  41.3 1.6 %collective-permute-start.6 = (f32[1,256,512]{2,1,0:T(8,128)S(1)}, f32[1,256,512]{2,1,0:T(8,128)S(1)}, u32[]{:S(2)}, u32[]{:S(2)}) collective-permute-start(f32[1,256,512]{2,1,0:T(8,128)S(1)} %get-tuple-element.38), channel_id=1, source_target_pairs={{0,2},{2,0},{1,3},{3,1},{4,6},{6,4},{5,7},{7,5},{8,10},{10,8},{9,1... | collective-permute-start | bytes 1572872 | tf_op jit(solution)/shard_map/ppermute | solution.py:496
  42.9 0.7 %collective-permute-done.4.rest_2_ = bf16[2,2,32768]{2,1,0:T(2,128)(2,1)S(1)} collective-permute-done((bf16[2,2,32768]{2,1,0:T(2,128)(2,1)S(1)}, bf16[2,2,32768]{2,1,0:T(2,128)(2,1)S(1)}, u32[]{:S(2)}, u32[]{:S(2)}) %collective-permute-start.4) | collective-permute-done | bytes 262176 | tf_op jit(solution)/shard_map/ppermute | solution.py:496
  43.6 10.5 %fine.1 = (f32[128,128]{1,0:T(8,128)S(1)}, f32[1,128,128]{2,1,0:T(8,128)S(1)}) custom-call(s32[4]{0:T(128)S(1)} %pad_add_fusion.info_ref, f32[1,32768]{1,0:T(1,128)S(1)} %bitcast.10, s32[8,128]{1,0:T(8,128)S(1)} %get-tuple-element.24.mult_ref, bf16[2,1,64,32768]{3,2,1,0:T(8,128)(2,1)} %g_ref.3, bf16[2,2,32768]{2,1,0:T(2,128)(2,1)S(1)} %get-tuple-element.30.rest_0_, ...), custom_call_target="tpu_custom_call" | custom-call | flops 2147483648 | bytes 8388608 | tf_op jit(solution)/shard_map/fine/pallas_call | solution.py:461
  54.1 1.6 %collective-permute-start.8 = (f32[1,128,128]{2,1,0:T(8,128)S(1)}, f32[1,128,128]{2,1,0:T(8,128)S(1)}, u32[]{:S(2)}, u32[]{:S(2)}) collective-permute-start(f32[1,128,128]{2,1,0:T(8,128)S(1)} %get-tuple-element.41), channel_id=1, source_target_pairs={{0,2},{2,0},{1,3},{3,1},{4,6},{6,4},{5,7},{7,5},{8,10},{10,8},{9,1... | collective-permute-start | bytes 196616 | tf_op jit(solution)/shard_map/ppermute | solution.py:496
  56.2 3.1 %collective-permute-done.7.rest_1_ = f32[1,8,128]{2,1,0:T(8,128)S(1)} collective-permute-done((f32[1,8,128]{2,1,0:T(8,128)S(1)}, f32[1,8,128]{2,1,0:T(8,128)S(1)}, u32[]{:S(2)}, u32[]{:S(2)}) %collective-permute-start.7) | collective-permute-done | bytes 4128 | tf_op jit(solution)/shard_map/ppermute | solution.py:496
  59.3 0.9 %coarse_final.1 = f32[16,256]{1,0:T(8,128)} custom-call(f32[256,512]{1,0:T(8,128)S(1)} %get-tuple-element.37.keep_ref, f32[8,128]{1,0:T(8,128)S(1)} %get-tuple-element.26.norm_ref, f32[1,256,512]{2,1,0:T(8,128)S(1)} %collective-permute-done.6.rest_0_, f32[1,8,128]{2,1,0:T(8,128)S(1)} %collective-permute-done.7.rest_1_), custom_call_target="tpu_custom_call" | custom-call | tf_op jit(solution)/shard_map/coarse_final/pallas_call | solution.py:597
  60.3 3.5 %collective-permute-start.9 = (f32[2,128]{1,0:T(2,128)S(1)}, f32[2,128]{1,0:T(2,128)S(1)}, u32[]{:S(2)}, u32[]{:S(2)}) collective-permute-start(f32[2,128]{1,0:T(2,128)S(1)} %get-tuple-element.43), channel_id=1, source_target_pairs={{0,12},{4,0},{8,4},{12,8},{1,13},{5,1},{9,5},{13,9},{2,14},{6,2},{... | collective-permute-start | bytes 3080 | tf_op jit(solution)/shard_map/ppermute | solution.py:496
  63.7 0.6 collective-permute-start.11
  64.4 0.7 collective-permute-done.9.rest_1_
  65.0 3.2 %collective-permute-done.10.rest_2_ = f32[2,128]{1,0:T(2,128)S(1)} collective-permute-done((f32[2,128]{1,0:T(2,128)S(1)}, f32[2,128]{1,0:T(2,128)S(1)}, u32[]{:S(2)}, u32[]{:S(2)}) %collective-permute-start.10) | collective-permute-done | bytes 1056 | tf_op jit(solution)/shard_map/ppermute | solution.py:496
  68.2 0.9 %collective-permute-done.11.rest_3_ = f32[2,128]{1,0:T(2,128)S(1)} collective-permute-done((f32[2,128]{1,0:T(2,128)S(1)}, f32[2,128]{1,0:T(2,128)S(1)}, u32[]{:S(2)}, u32[]{:S(2)}) %collective-permute-start.11) | collective-permute-done | bytes 1056 | tf_op jit(solution)/shard_map/ppermute | solution.py:496
  69.1 1.2 %place.1 = f32[4,2,32]{2,1,0:T(2,128)} custom-call(s32[4]{0:T(128)S(1)} %pad_add_fusion.info_ref, s32[2,16]{1,0:T(2,128)S(1)} %bitcast.14, f32[2,128]{1,0:T(2,128)S(1)} %get-tuple-element.42.rest_0_, f32[2,128]{1,0:T(2,128)S(1)} %collective-permute-done.9.rest_1_, f32[2,128]{1,0:T(2,128)S(1)} %collective-permute-done.10.rest_2_, ...), custom_call_target="tpu_custom_call" | custom-call | tf_op jit(solution)/shard_map/place/pallas_call | solution.py:613
  (25 shorter events, 1.0 us)
Async XLA Ops:
  0.6 25.0 %collective-permute-start.2 = (bf16[4,2,8192]{2,1,0:T(2,128)(2,1)}, bf16[4,2,8192]{2,1,0:T(2,128)(2,1)S(1)}, u32[]{:S(2)}, u32[]{:S(2)}) collective-permute-start(bf16[4,2,8192]{2,1,0:T(2,128)(2,1)} %rest_0_.1), channel_id=1, source_target_pairs={{0,12},{4,0},{8,4},{12,8},{1,13},{5,1},{9,5},{13,9},{2,14},{6,2},{... | collective-permute-start | bytes 393224 | tf_op jit(solution)/shard_map/ppermute | solution.py:496
  5.8 19.9 %collective-permute-start.1 = (bf16[4,2,8192]{2,1,0:T(2,128)(2,1)}, bf16[4,2,8192]{2,1,0:T(2,128)(2,1)S(1)}, u32[]{:S(2)}, u32[]{:S(2)}) collective-permute-start(bf16[4,2,8192]{2,1,0:T(2,128)(2,1)} %rest_0_.1), channel_id=1, source_target_pairs={{0,8},{4,12},{8,0},{12,4},{1,9},{5,13},{9,1},{13,5},{2,10},{6,14},... | collective-permute-start | bytes 393224 | tf_op jit(solution)/shard_map/ppermute | solution.py:496
  5.8 19.9 %collective-permute-start = (bf16[4,2,8192]{2,1,0:T(2,128)(2,1)}, bf16[4,2,8192]{2,1,0:T(2,128)(2,1)S(1)}, u32[]{:S(2)}, u32[]{:S(2)}) collective-permute-start(bf16[4,2,8192]{2,1,0:T(2,128)(2,1)} %rest_0_.1), channel_id=1, source_target_pairs={{0,4},{4,8},{8,12},{12,0},{1,5},{5,9},{9,13},{13,1},{2,6},{6,10},{... | collective-permute-start | bytes 393224 | tf_op jit(solution)/shard_map/ppermute | solution.py:496
  6.8 1.0 %copy-start.2 = (bf16[4,2,32768]{2,1,0:T(2,128)(2,1)S(1)}, bf16[4,2,32768]{2,1,0:T(2,128)(2,1)}, u32[]{:S(2)}) copy-start(bf16[4,2,32768]{2,1,0:T(2,128)(2,1)} %spec_ref.1) | copy-start | bytes 1572868
  7.9 0.7 copy-start.4
  8.6 0.7 copy-start.6
  9.3 18.0 %copy-start.7 = (bf16[4,2,8192]{2,1,0:T(2,128)(2,1)S(1)}, bf16[4,2,8192]{2,1,0:T(2,128)(2,1)}, u32[]{:S(2)}) copy-start(bf16[4,2,8192]{2,1,0:T(2,128)(2,1)} %rest_0_.1) | copy-start | bytes 393220
  11.6 31.3 %collective-permute-start.3 = (bf16[2,2,32768]{2,1,0:T(2,128)(2,1)S(1)}, bf16[2,2,32768]{2,1,0:T(2,128)(2,1)S(1)}, u32[]{:S(2)}, u32[]{:S(2)}) collective-permute-start(bf16[2,2,32768]{2,1,0:T(2,128)(2,1)S(1)} %get-tuple-element.31), channel_id=1, source_target_pairs={{0,4},{4,8},{8,12},{12,0},{1,5},{5,9},{9,13},{13,1},{2,6},{6,10},{... | collective-permute-start | bytes 786440 | tf_op jit(solution)/shard_map/ppermute | solution.py:496
  14.2 0.9 %copy-start = (f32[32768]{0:T(1024)S(1)}, f32[32768]{0:T(1024)}, u32[]{:S(2)}) copy-start(f32[32768]{0:T(1024)} %param.13) | copy-start | bytes 393220
  15.1 0.8 %copy-start.3 = (f32[8192]{0:T(1024)S(1)}, f32[8192]{0:T(1024)}, u32[]{:S(2)}) copy-start(f32[8192]{0:T(1024)} %param.12) | copy-start | bytes 98308
  25.6 18.0 %copy-start.1 = (f32[32768]{0:T(1024)S(1)}, f32[32768]{0:T(1024)}, u32[]{:S(2)}) copy-start(f32[32768]{0:T(1024)} %param.13) | copy-start | bytes 393220
  25.7 43.4 %copy-start.5 = (s32[16,2]{0,1:T(2,128)S(1)}, s32[16,2]{0,1:T(2,128)}, u32[]{:S(2)}) copy-start(s32[16,2]{0,1:T(2,128)} %param.14) | copy-start | bytes 388
  25.7 17.2 %collective-permute-start.5 = (bf16[2,2,32768]{2,1,0:T(2,128)(2,1)S(1)}, bf16[2,2,32768]{2,1,0:T(2,128)(2,1)S(1)}, u32[]{:S(2)}, u32[]{:S(2)}) collective-permute-start(bf16[2,2,32768]{2,1,0:T(2,128)(2,1)S(1)} %get-tuple-element.35), channel_id=1, source_target_pairs={{0,12},{4,0},{8,4},{12,8},{1,13},{5,1},{9,5},{13,9},{2,14},{6,2},{... | collective-permute-start | bytes 786440 | tf_op jit(solution)/shard_map/ppermute | solution.py:496
  27.1 16.6 %collective-permute-start.4 = (bf16[2,2,32768]{2,1,0:T(2,128)(2,1)S(1)}, bf16[2,2,32768]{2,1,0:T(2,128)(2,1)S(1)}, u32[]{:S(2)}, u32[]{:S(2)}) collective-permute-start(bf16[2,2,32768]{2,1,0:T(2,128)(2,1)S(1)} %get-tuple-element.33), channel_id=1, source_target_pairs={{0,8},{4,12},{8,0},{12,4},{1,9},{5,13},{9,1},{13,5},{2,10},{6,14},... | collective-permute-start | bytes 786440 | tf_op jit(solution)/shard_map/ppermute | solution.py:496
  41.3 17.9 %collective-permute-start.6 = (f32[1,256,512]{2,1,0:T(8,128)S(1)}, f32[1,256,512]{2,1,0:T(8,128)S(1)}, u32[]{:S(2)}, u32[]{:S(2)}) collective-permute-start(f32[1,256,512]{2,1,0:T(8,128)S(1)} %get-tuple-element.38), channel_id=1, source_target_pairs={{0,2},{2,0},{1,3},{3,1},{4,6},{6,4},{5,7},{7,5},{8,10},{10,8},{9,1... | collective-permute-start | bytes 1572872 | tf_op jit(solution)/shard_map/ppermute | solution.py:496
  54.1 6.1 %collective-permute-start.8 = (f32[1,128,128]{2,1,0:T(8,128)S(1)}, f32[1,128,128]{2,1,0:T(8,128)S(1)}, u32[]{:S(2)}, u32[]{:S(2)}) collective-permute-start(f32[1,128,128]{2,1,0:T(8,128)S(1)} %get-tuple-element.41), channel_id=1, source_target_pairs={{0,2},{2,0},{1,3},{3,1},{4,6},{6,4},{5,7},{7,5},{8,10},{10,8},{9,1... | collective-permute-start | bytes 196616 | tf_op jit(solution)/shard_map/ppermute | solution.py:496
  55.7 3.6 %collective-permute-start.7 = (f32[1,8,128]{2,1,0:T(8,128)S(1)}, f32[1,8,128]{2,1,0:T(8,128)S(1)}, u32[]{:S(2)}, u32[]{:S(2)}) collective-permute-start(f32[1,8,128]{2,1,0:T(8,128)S(1)} %get-tuple-element.39), channel_id=1, source_target_pairs={{0,2},{2,0},{1,3},{3,1},{4,6},{6,4},{5,7},{7,5},{8,10},{10,8},{9,1... | collective-permute-start | bytes 12296 | tf_op jit(solution)/shard_map/ppermute | solution.py:496
  60.3 4.8 %collective-permute-start.9 = (f32[2,128]{1,0:T(2,128)S(1)}, f32[2,128]{1,0:T(2,128)S(1)}, u32[]{:S(2)}, u32[]{:S(2)}) collective-permute-start(f32[2,128]{1,0:T(2,128)S(1)} %get-tuple-element.43), channel_id=1, source_target_pairs={{0,12},{4,0},{8,4},{12,8},{1,13},{5,1},{9,5},{13,9},{2,14},{6,2},{... | collective-permute-start | bytes 3080 | tf_op jit(solution)/shard_map/ppermute | solution.py:496
  63.7 4.5 %collective-permute-start.10 = (f32[2,128]{1,0:T(2,128)S(1)}, f32[2,128]{1,0:T(2,128)S(1)}, u32[]{:S(2)}, u32[]{:S(2)}) collective-permute-start(f32[2,128]{1,0:T(2,128)S(1)} %get-tuple-element.44), channel_id=1, source_target_pairs={{0,8},{4,12},{8,0},{12,4},{1,9},{5,13},{9,1},{13,5},{2,10},{6,14},... | collective-permute-start | bytes 3080 | tf_op jit(solution)/shard_map/ppermute | solution.py:496
  63.7 5.4 %collective-permute-start.11 = (f32[2,128]{1,0:T(2,128)S(1)}, f32[2,128]{1,0:T(2,128)S(1)}, u32[]{:S(2)}, u32[]{:S(2)}) collective-permute-start(f32[2,128]{1,0:T(2,128)S(1)} %get-tuple-element.45), channel_id=1, source_target_pairs={{0,4},{4,8},{8,12},{12,0},{1,5},{5,9},{9,13},{13,1},{2,6},{6,10},{... | collective-permute-start | bytes 3080 | tf_op jit(solution)/shard_map/ppermute | solution.py:496

commit v4 on v3

--- a/solution.py
+++ b/solution.py
@@ -243,7 +243,7 @@
     return taken, found
 
 
-def pick_kernel(info_ref, trig_ref, off_ref, spec_ref, *rest, banks, segs, top):
+def pick_kernel(info_ref, trig_ref, spec_ref, *rest, banks, segs, top):
     out_refs = rest[:banks]
     mult_ref, sems = rest[banks:]
     bank = info_ref[1]
@@ -264,7 +264,7 @@
         source = lax.rem(bank - k + banks, banks)
         _, found = ranked_pairs(trig_ref, source * segs, segs, top, bank)
         for c in range(CAP):
-            offset = off_ref[lax.rem(found[c], top), source * segs + found[c] // top]
+            offset = trig_ref[top + lax.rem(found[c], top), source * segs + found[c] // top]
             mult = jnp.where(line == k * CAP + c, 2 * offset + (LAGS - 1), mult)
     mult_ref[...] = mult
     for copy in copies:
@@ -556,20 +556,20 @@
         shift_permute(coarse_spectra, "bank", banks, k) for k in range(1, banks)
     ]
 
+    named = jnp.concatenate([triggers.T, offsets.T], axis=0)
     *picked, mult = pl.pallas_call(
         functools.partial(pick_kernel, banks=banks, segs=segs, top=top),
-        in_specs=[SMEM, SMEM, SMEM, pl.BlockSpec(memory_space=pltpu.HBM)],
+        in_specs=[SMEM, SMEM, HBM],
         out_shape=[jax.ShapeDtypeStruct((CAP, 2, fine_bins), BF16) for _ in range(banks)]
         + [jax.ShapeDtypeStruct((banks * CAP, LANES), jnp.int32)],
         scratch_shapes=[pltpu.SemaphoreType.DMA((banks * CAP,))],
         compiler_params=params(),
         name="pick",
-    )(fine_info, triggers.T, offsets.T, fine_spectra)
+    )(fine_info, named, fine_spectra)
     order = sorted(range(banks), key=lambda k: min(k, banks - k))
     fine_blocks = {}
-    for place, k in enumerate(order):
-        block = picked[k] if place < 2 else after(picked[k], *coarse_blocks)
-        fine_blocks[k] = block if k == 0 else shift_permute(block, "bank", banks, k)
+    for k in order:
+        fine_blocks[k] = picked[k] if k == 0 else shift_permute(picked[k], "bank", banks, k)
 
     line = max(coarse_templates.shape[1] // freqs // LANES, 1)
 
@@ -617,7 +617,7 @@
         scratch_shapes=[pltpu.VMEM((banks * CAP, LANES), F32)],
         compiler_params=params(8),
         name="place",
-    )(fine_info, triggers.T, *back)
+    )(fine_info, named, *back)
     return (coarse_snr.T, fine_snr)
 
 

time: 70.6 us -> 69.8 us (0.989)
  waiting for transfers between devices: 8.56 us -> 6.75 us
  starting transfers between devices: 18 us -> 19.6 us
  local copies, waits for them, and re-layouts: 4.08 us -> 2.72 us
  other arithmetic: 0.15 us -> 0.86 us
    ppermute x12, waiting for transfers between devices: 8.56 us -> 6.75 us  [shift_permute(): lax.ppermute(value, axis, [(i, (i + by) % count) for i in range(count)])]
    ppermute x12, starting transfers between devices: 18 us -> 19.6 us  [shift_permute(): lax.ppermute(value, axis, [(i, (i + by) % count) for i in range(count)])]
    unnamed x16 -> x10, local copies, waits for them, and re-layouts: 4.08 us -> 2.72 us
  transfers between devices with their start and end apart: 12 -> 12, of which waited for: 5 -> 3; matrix products, arithmetic and copies ran while one was open for 0% -> 1% of each run, Pallas kernels for 53% -> 54%
where the time goes in v4:
time: 69.8 us; the launch traced here: 69.6 us
  Pallas kernels  38.9 us (56%)
  starting transfers between devices  19.6 us (28%)
  waiting for transfers between devices  6.75 us (10%)
  local copies, waits for them, and re-layouts  2.72 us (4%)
  other arithmetic  0.86 us (1%)
  between operations  0.72 us (1%)
    ppermute x12, starting transfers between devices, shift_permute(): lax.ppermute(value, axis, [(i, (i + by) % count) for i in range(count)])  19.6 us
    pallas_call x1, Pallas kernels, coarse_section(): pl.pallas_call(kernel, in_specs=[SMEM, VMEM, HBM] + [VMEM for _ in blocks...  14.1 us
    pallas_call x1, Pallas kernels, fine_section(): pl.pallas_call(kernel, in_specs=[SMEM, VMEM, VMEM, HBM] + [VMEM for _ in...  10.5 us
    pallas_call x1, Pallas kernels, norm_section(): pl.pallas_call(functools.partial(norm_kernel, freqs=freqs), in_specs=[SME...  9.8 us
    ppermute x12, waiting for transfers between devices, shift_permute(): lax.ppermute(value, axis, [(i, (i + by) % count) for i in range(count)])  6.75 us
    unnamed x10, local copies, waits for them, and re-layouts  2.72 us
    pallas_call x1, Pallas kernels, body(): pl.pallas_call(functools.partial(pick_kernel, banks=banks, segs=segs, top...  2.3 us
  transfers between devices with their start and end apart: 12, of which 3 were waited for; matrix products, arithmetic and copies ran while one was open for 1% of the time, Pallas kernels for 54%

profile of v4, /device:TPU:0, one launch (start us, length us, event | category | flops | bytes accessed | tf_op | source)
XLA Modules:
  0.0 69.6 jit_solution(5884631922161194098)
XLA Ops:
  0.6 4.1 %collective-permute-start.1 = (bf16[4,2,8192]{2,1,0:T(2,128)(2,1)}, bf16[4,2,8192]{2,1,0:T(2,128)(2,1)S(1)}, u32[]{:S(2)}, u32[]{:S(2)}) collective-permute-start(bf16[4,2,8192]{2,1,0:T(2,128)(2,1)} %rest_0_.1), channel_id=1, source_target_pairs={{0,8},{4,12},{8,0},{12,4},{1,9},{5,13},{9,1},{13,5},{2,10},{6,14},... | collective-permute-start | bytes 393224 | tf_op jit(solution)/shard_map/ppermute | solution.py:496
  4.8 1.6 %collective-permute-start = (bf16[4,2,8192]{2,1,0:T(2,128)(2,1)}, bf16[4,2,8192]{2,1,0:T(2,128)(2,1)S(1)}, u32[]{:S(2)}, u32[]{:S(2)}) collective-permute-start(bf16[4,2,8192]{2,1,0:T(2,128)(2,1)} %rest_0_.1), channel_id=1, source_target_pairs={{0,4},{4,8},{8,12},{12,0},{1,5},{5,9},{9,13},{13,1},{2,6},{6,10},{... | collective-permute-start | bytes 393224 | tf_op jit(solution)/shard_map/ppermute | solution.py:496
  6.3 2.2 %collective-permute-start.2 = (bf16[4,2,8192]{2,1,0:T(2,128)(2,1)}, bf16[4,2,8192]{2,1,0:T(2,128)(2,1)S(1)}, u32[]{:S(2)}, u32[]{:S(2)}) collective-permute-start(bf16[4,2,8192]{2,1,0:T(2,128)(2,1)} %rest_0_.1), channel_id=1, source_target_pairs={{0,12},{4,0},{8,4},{12,8},{1,13},{5,1},{9,5},{13,9},{2,14},{6,2},{... | collective-permute-start | bytes 393224 | tf_op jit(solution)/shard_map/ppermute | solution.py:496
  8.6 0.7 %pad_add_fusion.trig_ref = s32[4,16]{1,0:T(4,128)S(1)} fusion(s32[2,16]{1,0:T(2,128)} %bitcast.14, s32[2,16]{1,0:T(2,128)} %bitcast.15), kind=kLoop, calls=%fused_computation | loop fusion | flops 64 | bytes 512 | tf_op jit(solution)/shard_map/concatenate | solution.py:559
  9.4 1.0 %copy-done.2 = bf16[4,2,32768]{2,1,0:T(2,128)(2,1)S(1)} copy-done((bf16[4,2,32768]{2,1,0:T(2,128)(2,1)S(1)}, bf16[4,2,32768]{2,1,0:T(2,128)(2,1)}, u32[]{:S(2)}) %copy-start.2) | copy-done | bytes 524312
  10.4 2.3 %pick.1 = (bf16[2,2,32768]{2,1,0:T(2,128)(2,1)S(1)}, bf16[2,2,32768]{2,1,0:T(2,128)(2,1)S(1)}, bf16[2,2,32768]{2,1,0:T(2,128)(2,1)S(1)}, bf16[2,2,32768]{2,1,0:T(2,128)(2,1)S(1)}, s32[8,128]{1,0:T(8,128)S(1)}) custom-call(s32[4]{0:T(128)S(1)} %pad_add_fusion.1.info_ref, s32[4,16]{1,0:T(4,128)S(1)} %pad_add_fusion.trig_ref, bf16[4,2,32768]{2,1,0:T(2,128)(2,1)S(1)} %copy-done.2), custom_call_target="tpu_custom_call" | custom-call | tf_op jit(solution)/shard_map/pick/pallas_call | solution.py:560
  12.8 0.6 collective-permute-start.4
  13.4 0.9 %copy-done = f32[32768]{0:T(1024)S(1)} copy-done((f32[32768]{0:T(1024)S(1)}, f32[32768]{0:T(1024)}, u32[]{:S(2)}) %copy-start) | copy-done | bytes 131096
  14.3 0.8 %copy-done.3 = f32[8192]{0:T(1024)S(1)} copy-done((f32[8192]{0:T(1024)S(1)}, f32[8192]{0:T(1024)}, u32[]{:S(2)}) %copy-start.3) | copy-done | bytes 32792
  15.1 9.8 %norms.1 = (f32[8,128]{1,0:T(8,128)S(1)}, f32[1,8,128]{2,1,0:T(8,128)S(1)}) custom-call(s32[4]{0:T(128)S(1)} %pad_add_fusion.2.info_ref, f32[1,8192]{1,0:T(1,128)S(1)} %bitcast.11, f32[1,32768]{1,0:T(1,128)S(1)} %bitcast.9, bf16[2,512,8192]{2,1,0:T(8,128)(2,1)} %h_ref.3, bf16[2,1,64,32768]{3,2,1,0:T(8,128)(2,1)} %g_ref.3), custom_call_target="tpu_custom_call" | custom-call | flops 1000000000 | bytes 25165824 | tf_op jit(solution)/shard_map/norms/pallas_call | solution.py:504
  24.9 3.3 %collective-permute-start.5 = (bf16[2,2,32768]{2,1,0:T(2,128)(2,1)S(1)}, bf16[2,2,32768]{2,1,0:T(2,128)(2,1)S(1)}, u32[]{:S(2)}, u32[]{:S(2)}) collective-permute-start(bf16[2,2,32768]{2,1,0:T(2,128)(2,1)S(1)} %get-tuple-element.31), channel_id=1, source_target_pairs={{0,12},{4,0},{8,4},{12,8},{1,13},{5,1},{9,5},{13,9},{2,14},{6,2},{... | collective-permute-start | bytes 786440 | tf_op jit(solution)/shard_map/ppermute | solution.py:496
  28.2 14.1 %coarse.1 = (f32[256,512]{1,0:T(8,128)S(1)}, f32[1,256,512]{2,1,0:T(8,128)S(1)}) custom-call(s32[4]{0:T(128)S(1)} %pad_add_fusion.2.info_ref, f32[1,8192]{1,0:T(1,128)S(1)} %bitcast.12, bf16[2,512,8192]{2,1,0:T(8,128)(2,1)} %h_ref.3, bf16[4,2,8192]{2,1,0:T(2,128)(2,1)S(1)} %copy-done.4, bf16[4,2,8192]{2,1,0:T(2,128)(2,1)S(1)} %collective-permute-done.rest_1_, ...), custom_call_target="tpu_custom_call" | custom-call | flops 8589934592 | bytes 16777216 | tf_op jit(solution)/shard_map/coarse/pallas_call | solution.py:421
  42.3 1.6 %collective-permute-start.6 = (f32[1,256,512]{2,1,0:T(8,128)S(1)}, f32[1,256,512]{2,1,0:T(8,128)S(1)}, u32[]{:S(2)}, u32[]{:S(2)}) collective-permute-start(f32[1,256,512]{2,1,0:T(8,128)S(1)} %get-tuple-element.34), channel_id=1, source_target_pairs={{0,2},{2,0},{1,3},{3,1},{4,6},{6,4},{5,7},{7,5},{8,10},{10,8},{9,1... | collective-permute-start | bytes 1572872 | tf_op jit(solution)/shard_map/ppermute | solution.py:496
  43.9 10.5 %fine.1 = (f32[128,128]{1,0:T(8,128)S(1)}, f32[1,128,128]{2,1,0:T(8,128)S(1)}) custom-call(s32[4]{0:T(128)S(1)} %pad_add_fusion.1.info_ref, f32[1,32768]{1,0:T(1,128)S(1)} %bitcast.10, s32[8,128]{1,0:T(8,128)S(1)} %get-tuple-element.22.mult_ref, bf16[2,1,64,32768]{3,2,1,0:T(8,128)(2,1)} %g_ref.3, bf16[2,2,32768]{2,1,0:T(2,128)(2,1)S(1)} %get-tuple-element.28.rest_0_, ...), custom_call_target="tpu_custom_call" | custom-call | flops 2147483648 | bytes 8388608 | tf_op jit(solution)/shard_map/fine/pallas_call | solution.py:461
  54.4 0.6 collective-permute-start.8
  55.0 1.5 %collective-permute-start.7 = (f32[1,8,128]{2,1,0:T(8,128)S(1)}, f32[1,8,128]{2,1,0:T(8,128)S(1)}, u32[]{:S(2)}, u32[]{:S(2)}) collective-permute-start(f32[1,8,128]{2,1,0:T(8,128)S(1)} %get-tuple-element.35), channel_id=1, source_target_pairs={{0,2},{2,0},{1,3},{3,1},{4,6},{6,4},{5,7},{7,5},{8,10},{10,8},{9,1... | collective-permute-start | bytes 12296 | tf_op jit(solution)/shard_map/ppermute | solution.py:496
  56.5 2.3 %collective-permute-done.7.rest_1_ = f32[1,8,128]{2,1,0:T(8,128)S(1)} collective-permute-done((f32[1,8,128]{2,1,0:T(8,128)S(1)}, f32[1,8,128]{2,1,0:T(8,128)S(1)}, u32[]{:S(2)}, u32[]{:S(2)}) %collective-permute-start.7) | collective-permute-done | bytes 4128 | tf_op jit(solution)/shard_map/ppermute | solution.py:496
  58.8 0.9 %coarse_final.1 = f32[16,256]{1,0:T(8,128)} custom-call(f32[256,512]{1,0:T(8,128)S(1)} %get-tuple-element.33.keep_ref, f32[8,128]{1,0:T(8,128)S(1)} %get-tuple-element.24.norm_ref, f32[1,256,512]{2,1,0:T(8,128)S(1)} %collective-permute-done.6.rest_0_, f32[1,8,128]{2,1,0:T(8,128)S(1)} %collective-permute-done.7.rest_1_), custom_call_target="tpu_custom_call" | custom-call | tf_op jit(solution)/shard_map/coarse_final/pallas_call | solution.py:597
  59.8 0.7 collective-permute-start.9
  60.5 2.5 %collective-permute-start.10 = (f32[2,128]{1,0:T(2,128)S(1)}, f32[2,128]{1,0:T(2,128)S(1)}, u32[]{:S(2)}, u32[]{:S(2)}) collective-permute-start(f32[2,128]{1,0:T(2,128)S(1)} %get-tuple-element.40), channel_id=1, source_target_pairs={{0,8},{4,12},{8,0},{12,4},{1,9},{5,13},{9,1},{13,5},{2,10},{6,14},... | collective-permute-start | bytes 3080 | tf_op jit(solution)/shard_map/ppermute | solution.py:496
  63.0 0.9 %collective-permute-start.11 = (f32[2,128]{1,0:T(2,128)S(1)}, f32[2,128]{1,0:T(2,128)S(1)}, u32[]{:S(2)}, u32[]{:S(2)}) collective-permute-start(f32[2,128]{1,0:T(2,128)S(1)} %get-tuple-element.41), channel_id=1, source_target_pairs={{0,4},{4,8},{8,12},{12,0},{1,5},{5,9},{9,13},{13,1},{2,6},{6,10},{... | collective-permute-start | bytes 3080 | tf_op jit(solution)/shard_map/ppermute | solution.py:496
  63.9 1.0 %collective-permute-done.10.rest_2_ = f32[2,128]{1,0:T(2,128)S(1)} collective-permute-done((f32[2,128]{1,0:T(2,128)S(1)}, f32[2,128]{1,0:T(2,128)S(1)}, u32[]{:S(2)}, u32[]{:S(2)}) %collective-permute-start.10) | collective-permute-done | bytes 1056 | tf_op jit(solution)/shard_map/ppermute | solution.py:496
  64.9 3.4 %collective-permute-done.11.rest_3_ = f32[2,128]{1,0:T(2,128)S(1)} collective-permute-done((f32[2,128]{1,0:T(2,128)S(1)}, f32[2,128]{1,0:T(2,128)S(1)}, u32[]{:S(2)}, u32[]{:S(2)}) %collective-permute-start.11) | collective-permute-done | bytes 1056 | tf_op jit(solution)/shard_map/ppermute | solution.py:496
  68.3 1.2 %place.1 = f32[4,2,32]{2,1,0:T(2,128)} custom-call(s32[4]{0:T(128)S(1)} %pad_add_fusion.1.info_ref, s32[4,16]{1,0:T(4,128)S(1)} %pad_add_fusion.trig_ref, f32[2,128]{1,0:T(2,128)S(1)} %get-tuple-element.38.rest_0_, f32[2,128]{1,0:T(2,128)S(1)} %collective-permute-done.9.rest_1_, f32[2,128]{1,0:T(2,128)S(1)} %collective-permute-done.10.rest_2_, ...), custom_call_target="tpu_custom_call" | custom-call | tf_op jit(solution)/shard_map/place/pallas_call | solution.py:613
  (20 shorter events, 0.3 us)
Async XLA Ops:
  0.6 24.3 %collective-permute-start.1 = (bf16[4,2,8192]{2,1,0:T(2,128)(2,1)}, bf16[4,2,8192]{2,1,0:T(2,128)(2,1)S(1)}, u32[]{:S(2)}, u32[]{:S(2)}) collective-permute-start(bf16[4,2,8192]{2,1,0:T(2,128)(2,1)} %rest_0_.1), channel_id=1, source_target_pairs={{0,8},{4,12},{8,0},{12,4},{1,9},{5,13},{9,1},{13,5},{2,10},{6,14},... | collective-permute-start | bytes 393224 | tf_op jit(solution)/shard_map/ppermute | solution.py:496
  4.8 23.5 %collective-permute-start = (bf16[4,2,8192]{2,1,0:T(2,128)(2,1)}, bf16[4,2,8192]{2,1,0:T(2,128)(2,1)S(1)}, u32[]{:S(2)}, u32[]{:S(2)}) collective-permute-start(bf16[4,2,8192]{2,1,0:T(2,128)(2,1)} %rest_0_.1), channel_id=1, source_target_pairs={{0,4},{4,8},{8,12},{12,0},{1,5},{5,9},{9,13},{13,1},{2,6},{6,10},{... | collective-permute-start | bytes 393224 | tf_op jit(solution)/shard_map/ppermute | solution.py:496
  6.3 21.9 %collective-permute-start.2 = (bf16[4,2,8192]{2,1,0:T(2,128)(2,1)}, bf16[4,2,8192]{2,1,0:T(2,128)(2,1)S(1)}, u32[]{:S(2)}, u32[]{:S(2)}) collective-permute-start(bf16[4,2,8192]{2,1,0:T(2,128)(2,1)} %rest_0_.1), channel_id=1, source_target_pairs={{0,12},{4,0},{8,4},{12,8},{1,13},{5,1},{9,5},{13,9},{2,14},{6,2},{... | collective-permute-start | bytes 393224 | tf_op jit(solution)/shard_map/ppermute | solution.py:496
  9.4 1.0 %copy-start.2 = (bf16[4,2,32768]{2,1,0:T(2,128)(2,1)S(1)}, bf16[4,2,32768]{2,1,0:T(2,128)(2,1)}, u32[]{:S(2)}) copy-start(bf16[4,2,32768]{2,1,0:T(2,128)(2,1)} %spec_ref.1) | copy-start | bytes 1572868
  10.4 17.8 %copy-start.4 = (bf16[4,2,8192]{2,1,0:T(2,128)(2,1)S(1)}, bf16[4,2,8192]{2,1,0:T(2,128)(2,1)}, u32[]{:S(2)}) copy-start(bf16[4,2,8192]{2,1,0:T(2,128)(2,1)} %rest_0_.1) | copy-start | bytes 393220
  12.7 31.2 %collective-permute-start.3 = (bf16[2,2,32768]{2,1,0:T(2,128)(2,1)S(1)}, bf16[2,2,32768]{2,1,0:T(2,128)(2,1)S(1)}, u32[]{:S(2)}, u32[]{:S(2)}) collective-permute-start(bf16[2,2,32768]{2,1,0:T(2,128)(2,1)S(1)} %get-tuple-element.29), channel_id=1, source_target_pairs={{0,4},{4,8},{8,12},{12,0},{1,5},{5,9},{9,13},{13,1},{2,6},{6,10},{... | collective-permute-start | bytes 786440 | tf_op jit(solution)/shard_map/ppermute | solution.py:496
  12.8 31.1 %collective-permute-start.4 = (bf16[2,2,32768]{2,1,0:T(2,128)(2,1)S(1)}, bf16[2,2,32768]{2,1,0:T(2,128)(2,1)S(1)}, u32[]{:S(2)}, u32[]{:S(2)}) collective-permute-start(bf16[2,2,32768]{2,1,0:T(2,128)(2,1)S(1)} %get-tuple-element.30), channel_id=1, source_target_pairs={{0,8},{4,12},{8,0},{12,4},{1,9},{5,13},{9,1},{13,5},{2,10},{6,14},... | collective-permute-start | bytes 786440 | tf_op jit(solution)/shard_map/ppermute | solution.py:496
  13.4 0.9 %copy-start = (f32[32768]{0:T(1024)S(1)}, f32[32768]{0:T(1024)}, u32[]{:S(2)}) copy-start(f32[32768]{0:T(1024)} %param.13) | copy-start | bytes 393220
  14.3 0.8 %copy-start.3 = (f32[8192]{0:T(1024)S(1)}, f32[8192]{0:T(1024)}, u32[]{:S(2)}) copy-start(f32[8192]{0:T(1024)} %param.12) | copy-start | bytes 98308
  24.9 19.0 %copy-start.1 = (f32[32768]{0:T(1024)S(1)}, f32[32768]{0:T(1024)}, u32[]{:S(2)}) copy-start(f32[32768]{0:T(1024)} %param.13) | copy-start | bytes 393220
  24.9 19.0 %collective-permute-start.5 = (bf16[2,2,32768]{2,1,0:T(2,128)(2,1)S(1)}, bf16[2,2,32768]{2,1,0:T(2,128)(2,1)S(1)}, u32[]{:S(2)}, u32[]{:S(2)}) collective-permute-start(bf16[2,2,32768]{2,1,0:T(2,128)(2,1)S(1)} %get-tuple-element.31), channel_id=1, source_target_pairs={{0,12},{4,0},{8,4},{12,8},{1,13},{5,1},{9,5},{13,9},{2,14},{6,2},{... | collective-permute-start | bytes 786440 | tf_op jit(solution)/shard_map/ppermute | solution.py:496
  42.3 16.4 %collective-permute-start.6 = (f32[1,256,512]{2,1,0:T(8,128)S(1)}, f32[1,256,512]{2,1,0:T(8,128)S(1)}, u32[]{:S(2)}, u32[]{:S(2)}) collective-permute-start(f32[1,256,512]{2,1,0:T(8,128)S(1)} %get-tuple-element.34), channel_id=1, source_target_pairs={{0,2},{2,0},{1,3},{3,1},{4,6},{6,4},{5,7},{7,5},{8,10},{10,8},{9,1... | collective-permute-start | bytes 1572872 | tf_op jit(solution)/shard_map/ppermute | solution.py:496
  54.4 5.3 %collective-permute-start.8 = (f32[1,128,128]{2,1,0:T(8,128)S(1)}, f32[1,128,128]{2,1,0:T(8,128)S(1)}, u32[]{:S(2)}, u32[]{:S(2)}) collective-permute-start(f32[1,128,128]{2,1,0:T(8,128)S(1)} %get-tuple-element.37), channel_id=1, source_target_pairs={{0,2},{2,0},{1,3},{3,1},{4,6},{6,4},{5,7},{7,5},{8,10},{10,8},{9,1... | collective-permute-start | bytes 196616 | tf_op jit(solution)/shard_map/ppermute | solution.py:496
  55.0 3.8 %collective-permute-start.7 = (f32[1,8,128]{2,1,0:T(8,128)S(1)}, f32[1,8,128]{2,1,0:T(8,128)S(1)}, u32[]{:S(2)}, u32[]{:S(2)}) collective-permute-start(f32[1,8,128]{2,1,0:T(8,128)S(1)} %get-tuple-element.35), channel_id=1, source_target_pairs={{0,2},{2,0},{1,3},{3,1},{4,6},{6,4},{5,7},{7,5},{8,10},{10,8},{9,1... | collective-permute-start | bytes 12296 | tf_op jit(solution)/shard_map/ppermute | solution.py:496
  59.8 4.1 %collective-permute-start.9 = (f32[2,128]{1,0:T(2,128)S(1)}, f32[2,128]{1,0:T(2,128)S(1)}, u32[]{:S(2)}, u32[]{:S(2)}) collective-permute-start(f32[2,128]{1,0:T(2,128)S(1)} %get-tuple-element.39), channel_id=1, source_target_pairs={{0,12},{4,0},{8,4},{12,8},{1,13},{5,1},{9,5},{13,9},{2,14},{6,2},{... | collective-permute-start | bytes 3080 | tf_op jit(solution)/shard_map/ppermute | solution.py:496
  60.5 4.5 %collective-permute-start.10 = (f32[2,128]{1,0:T(2,128)S(1)}, f32[2,128]{1,0:T(2,128)S(1)}, u32[]{:S(2)}, u32[]{:S(2)}) collective-permute-start(f32[2,128]{1,0:T(2,128)S(1)} %get-tuple-element.40), channel_id=1, source_target_pairs={{0,8},{4,12},{8,0},{12,4},{1,9},{5,13},{9,1},{13,5},{2,10},{6,14},... | collective-permute-start | bytes 3080 | tf_op jit(solution)/shard_map/ppermute | solution.py:496
  63.0 5.4 %collective-permute-start.11 = (f32[2,128]{1,0:T(2,128)S(1)}, f32[2,128]{1,0:T(2,128)S(1)}, u32[]{:S(2)}, u32[]{:S(2)}) collective-permute-start(f32[2,128]{1,0:T(2,128)S(1)} %get-tuple-element.41), channel_id=1, source_target_pairs={{0,4},{4,8},{8,12},{12,0},{1,5},{5,9},{9,13},{13,1},{2,6},{6,10},{... | collective-permute-start | bytes 3080 | tf_op jit(solution)/shard_map/ppermute | solution.py:496
